TPU v7x, 32 devices: a whole 2x2x4 slice. The times are simulated.
32 devices in a mesh: dp: 4 (over z), row: 2 (over y), col: 4 (over x, core).
Axes of the slice: x: 2, y: 2, z: 4, core: 2. Of those that a mesh axis runs over, the one named last changes fastest.
Arguments:
- activations: bfloat16 [4096, 4096], P('dp', 'col'), may hold values from -6 to 6
- out_grad: bfloat16 [4096, 14336], P('dp', 'row'), may hold values from -6 to 6
- weight: float32 [2, 7168, 4096], P('row', 'dp', 'col'), as said below
- step_size: float32 [2, 7168], P('row'), may hold values from 0.001 to 0.016
Outputs:
- input_grad: bfloat16 [4096, 4096], P(('dp', 'row'), 'col')
- weight_grad: float32 [2, 7168, 4096], P('row', 'dp', 'col')
- step_grad: float32 [2, 7168], P('row', 'dp')
Inputs may be any that keep to these rules, and one draw needn't show every extreme that they name: Each latent weight divided by its row's step lies at least 0.1 away from every multiple of one half.
All inputs are finite; a program needn't handle non-finite values.
Results may differ from a plain program's by a relative error of at most 0.0096.
Values may be sent and summed in bfloat16 or wider, within the bound.
A program may use at most 128 MiB of HBM per device.

v0:
```python
import jax
import jax.numpy as jnp
from jax import lax
from jax.experimental.layout import Layout, with_layout_constraint
from jax.sharding import PartitionSpec as P

D = 4096


def quantize(latent, scales):
    ratio = latent / scales[:, None]
    clipped = jnp.clip(ratio, -8.0, 7.0)
    levels = jnp.floor(clipped + 0.5)
    inside = jnp.where((ratio >= -8.0) & (ratio <= 7.0), 1.0, 0.0).astype(jnp.float32)
    factor = jnp.where(inside > 0.5, levels - ratio, clipped)
    quantized = (levels * scales[:, None]).astype(jnp.bfloat16)
    return (quantized, inside, factor)


def shift(block, axis, count, by):
    return lax.ppermute(block, axis, [(i, (i + by) % count) for i in range(count)])


def swap(block, axis, count, bit):
    return lax.ppermute(block, axis, [(i, i ^ bit) for i in range(count)])


def gather_rows(block, axis, count):
    position = lax.axis_index(axis)
    bit = 1
    bits = []
    while bit < count:
        bits.append(bit)
        bit *= 2
    pieces = {0: block}
    for bit in reversed(bits):
        held = dict(pieces)
        for key in held:
            pieces[key ^ bit] = swap(held[key], axis, count, bit)
    parts = [pieces[key] for key in range(count)]
    for bit in bits:
        flag = (position & bit) != 0
        parts = [
            jnp.where(flag, parts[key ^ bit], parts[key]) for key in range(count)
        ]
    return jnp.concatenate(parts, axis=0)


def make_shards(n_dp, n_row, n_col):
    def shards(activations, out_grad, weight, step_size):
        own_count = weight.shape[1]
        tokens = out_grad.shape[0]
        dp = lax.axis_index("dp")
        row = lax.axis_index("row")
        col = lax.axis_index("col")
        scales = step_size[0]
        own_scales = lax.dynamic_slice_in_dim(scales, dp * own_count, own_count, 0)
        grad_factor = 1.0 / (7.0 * D) ** 0.5

        share = tokens // n_col
        half = tokens // n_row
        mine = lax.dynamic_slice_in_dim(out_grad, col * share, share, 0)
        ring = lax.dynamic_slice_in_dim(activations, row * half, half, 0)
        grads, acts = [], []
        for k in range(1, n_dp):
            target = (dp + k) % n_dp
            chunk = lax.dynamic_slice_in_dim(mine, target * own_count, own_count, 1)
            grads.append(shift(chunk, "dp", n_dp, k))
            ring = shift(ring, "dp", n_dp, 1)
            acts.append(ring)

        quantized, _, _ = quantize(weight[0], own_scales)
        own_grad = lax.dynamic_slice_in_dim(out_grad, dp * own_count, own_count, 1)

        def reduced(grad):
            size = tokens
            bit = n_row // 2
            if bit == 0:
                return jnp.dot(grad, quantized, preferred_element_type=jnp.float32)
            size //= 2
            upper = ((row // bit) % 2).astype(jnp.int32)
            sent = lax.dynamic_slice_in_dim(grad, (1 - upper) * size, size, 0)
            kept = lax.dynamic_slice_in_dim(grad, upper * size, size, 0)
            out = jnp.dot(sent, quantized, preferred_element_type=jnp.float32).astype(jnp.bfloat16)
            came = swap(out, "row", n_row, bit)
            total = jnp.dot(kept, quantized, preferred_element_type=jnp.float32) + came.astype(jnp.float32)
            bit //= 2
            while bit:
                size //= 2
                upper = (row // bit) % 2 == 1
                low, high = total[:size], total[size:]
                came = swap(jnp.where(upper, low, high).astype(jnp.bfloat16), "row", n_row, bit)
                total = jnp.where(upper, high, low) + came.astype(jnp.float32)
                bit //= 2
            return total

        products = lax.dot_general(
            own_grad, activations, (((0,), (0,)), ((), ())), preferred_element_type=jnp.float32
        )
        own_total = reduced(own_grad)
        if grads:
            grads[0], quantized, products = lax.optimization_barrier((grads[0], quantized, products))
        running = None
        for k in range(1, n_dp):
            grad = gather_rows(grads[k - 1], "col", n_col)
            total = reduced(grad)
            if running is not None:
                total = total + running.astype(jnp.float32)
            leaving, grad = lax.optimization_barrier((total.astype(jnp.bfloat16), grad))
            running = shift(leaving, "dp", n_dp, 1)
            act = gather_rows(acts[k - 1], "row", n_row)
            products = products + lax.dot_general(
                grad, act, (((0,), (0,)), ((), ())), preferred_element_type=jnp.float32
            )
        if running is not None:
            own_total = own_total + running.astype(jnp.float32)
        products, latent = lax.optimization_barrier((products, weight[0]))
        products = with_layout_constraint(products, Layout((0, 1)))
        _, inside, factor = quantize(latent, own_scales)
        input_grad = own_total.astype(jnp.bfloat16)
        step_rows = lax.psum(jnp.sum(products * factor, axis=1) * grad_factor, "col")
        weight_grad = (products * inside)[None]
        return (input_grad, weight_grad, step_rows[None])

    return shards


def solution(mesh):
    in_specs = (P("dp", "col"), P("dp", "row"), P("row", "dp", "col"), P("row", None))
    out_specs = (P(("dp", "row"), "col"), P("row", "dp", "col"), P("row", "dp"))
    shards = make_shards(mesh.shape["dp"], mesh.shape["row"], mesh.shape["col"])
    return jax.shard_map(shards, mesh=mesh, in_specs=in_specs, out_specs=out_specs, check_vma=False)
```

profile of v0, /device:TPU:0, one launch (start us, length us, event | category | flops | bytes accessed | tf_op | source)
XLA Modules:
  0.0 320.4 jit_solution(8986064453611099961)
XLA Ops:
  0.7 5.1 %fusion.58 = (bf16[256,1792]{1,0:T(8,128)(2,1)}, bf16[256,1792]{1,0:T(8,128)(2,1)}, bf16[256,1792]{1,0:T(8,128)(2,1)}) fusion(bf16[1024,7168]{1,0:T(8,128)(2,1)} %param.5, s32[]{:T(128)S(6)} %select_n.223, s32[]{:T(128)S(6)} %select_n.226, s32[]{:T(128)S(6)} %select_n.237, s32[]{:T(128)S(6)} %select_n.240), kind=kLoop, calls=%fused_computation.91 | loop fusion | bytes 5505040 | tf_op jit(solution)/shard_map/dynamic_slice | solution.py:67
  5.9 3.0 collective-permute-start.5
  12.4 5.2 %multiply_convert_fusion = bf16[1792,1024]{1,0:T(8,128)(2,1)} fusion(f32[1792]{0:T(1024)S(1)} %dynamic-slice_reduce_fusion, f32[1,1792,1024]{2,1,0:T(8,128)} %param.6), kind=kLoop, calls=%fused_computation.5 | loop fusion | flops 11010048 | bytes 11017216 | tf_op jit(solution)/shard_map/convert_element_type | solution.py:16
  17.6 8.1 %fusion.1 = f32[1792,1024]{1,0:T(8,128)} fusion(bf16[1024,1024]{1,0:T(8,128)(2,1)S(1)} %copy-done, bf16[1024,7168]{1,0:T(8,128)(2,1)} %param.5, s32[]{:T(128)S(6)} %select_n.216), kind=kOutput, calls=%fused_computation.10 | convolution fusion | flops 3758096384 | bytes 13107204 | tf_op jit(solution)/shard_map/dot_general | solution.py:97
  25.7 6.8 %collective-permute-done.5 = bf16[256,1792]{1,0:T(8,128)(2,1)} collective-permute-done((bf16[256,1792]{1,0:T(8,128)(2,1)}, bf16[256,1792]{1,0:T(8,128)(2,1)}, u32[]{:S(2)}, u32[]{:S(2)}) %collective-permute-start.5) | collective-permute-done | bytes 917536 | tf_op jit(solution)/shard_map/ppermute | solution.py:21
  36.6 57.0 %collective-permute-done.7 = bf16[256,1792]{1,0:T(8,128)(2,1)} collective-permute-done((bf16[256,1792]{1,0:T(8,128)(2,1)}, bf16[256,1792]{1,0:T(8,128)(2,1)}, u32[]{:S(2)}, u32[]{:S(2)}) %collective-permute-start.7) | collective-permute-done | bytes 917536 | tf_op jit(solution)/shard_map/ppermute | solution.py:21
  96.5 6.4 %fusion.28 = f32[512,1024]{1,0:T(8,128)} fusion(bf16[1792,1024]{1,0:T(8,128)(2,1)} %multiply_convert_fusion, bf16[1024,7168]{1,0:T(8,128)(2,1)} %param.5, s32[]{:T(128)S(6)} %select_n.215, s32[]{:T(128)S(6)} %select_n.217), kind=kOutput, calls=%fused_computation.42 | convolution fusion | flops 1879048192 | bytes 7602184 | tf_op jit(solution)/shard_map/dot_general | solution.py:86
  103.0 5.7 %fusion.30 = bf16[512,1024]{1,0:T(8,128)(2,1)} fusion(bf16[1792,1024]{1,0:T(8,128)(2,1)} %multiply_convert_fusion, bf16[1024,7168]{1,0:T(8,128)(2,1)} %param.5, s32[]{:T(128)S(6)} %select_n.219, s32[]{:T(128)S(6)} %select_n.217), kind=kOutput, calls=%fused_computation.44 | convolution fusion | flops 1879572480 | bytes 6553608 | tf_op jit(solution)/shard_map/dot_general | solution.py:84
  108.7 11.2 %collective-permute-done.20 = bf16[512,1024]{1,0:T(8,128)(2,1)S(1)} collective-permute-done((bf16[512,1024]{1,0:T(8,128)(2,1)}, bf16[512,1024]{1,0:T(8,128)(2,1)S(1)}, u32[]{:S(2)}, u32[]{:S(2)}) %collective-permute-start.20) | collective-permute-done | bytes 1048608 | tf_op jit(solution)/shard_map/ppermute | solution.py:25
  119.9 16.1 %collective-permute-start.21 = (bf16[512,1024]{1,0:T(8,128)(2,1)}, bf16[512,1024]{1,0:T(8,128)(2,1)S(1)}, u32[]{:S(2)}, u32[]{:S(2)}) collective-permute-start(bf16[512,1024]{1,0:T(8,128)(2,1)} %collective-permute-done.19), channel_id=1, source_target_pairs={{0,8},{8,16},{16,24},{24,0},{1,9},{9,17},{17,25},{25,1},{2,10},{10... | collective-permute-start | bytes 3145736 | tf_op jit(solution)/shard_map/ppermute | solution.py:21
  143.6 18.5 %collective-permute-done.2 = bf16[256,1792]{1,0:T(8,128)(2,1)S(1)} collective-permute-done((bf16[256,1792]{1,0:T(8,128)(2,1)}, bf16[256,1792]{1,0:T(8,128)(2,1)S(1)}, u32[]{:S(2)}, u32[]{:S(2)}) %collective-permute-start.2) | collective-permute-done | bytes 917536 | tf_op jit(solution)/shard_map/ppermute | solution.py:25
  177.4 12.2 %collective-permute-done.23 = bf16[512,1024]{1,0:T(8,128)(2,1)S(1)} collective-permute-done((bf16[512,1024]{1,0:T(8,128)(2,1)S(1)}, bf16[512,1024]{1,0:T(8,128)(2,1)S(1)}, u32[]{:S(2)}, u32[]{:S(2)}) %collective-permute-start.23) | collective-permute-done | bytes 1048608 | tf_op jit(solution)/shard_map/ppermute | solution.py:21
  191.2 19.4 %collective-permute-done.15 = bf16[512,1024]{1,0:T(8,128)(2,1)S(1)} collective-permute-done((bf16[512,1024]{1,0:T(8,128)(2,1)S(1)}, bf16[512,1024]{1,0:T(8,128)(2,1)S(1)}, u32[]{:S(2)}, u32[]{:S(2)}) %collective-permute-start.15) | collective-permute-done | bytes 1048608 | tf_op jit(solution)/shard_map/ppermute | solution.py:25
  213.1 2.6 collective-permute-start.16
  215.9 6.1 %fusion.3 = f32[1792,1024]{1,0:T(8,128)} fusion(bf16[1024,1792]{1,0:T(8,128)(2,1)S(1)} %pad_maximum_fusion.2, bf16[512,1024]{1,0:T(8,128)(2,1)S(1)} %get-tuple-element.45, bf16[512,1024]{1,0:T(8,128)(2,1)S(1)} %get-tuple-element.44), kind=kOutput, calls=%fused_computation.13 | convolution fusion | flops 3762290688 | bytes 13107200 | tf_op jit(solution)/shard_map/dot_general | solution.py:112
  222.0 11.0 %collective-permute-done.11 = bf16[512,1024]{1,0:T(8,128)(2,1)S(1)} collective-permute-done((bf16[512,1024]{1,0:T(8,128)(2,1)S(1)}, bf16[512,1024]{1,0:T(8,128)(2,1)S(1)}, u32[]{:S(2)}, u32[]{:S(2)}) %collective-permute-start.11) | collective-permute-done | bytes 1048608 | tf_op jit(solution)/shard_map/ppermute | solution.py:25
  233.0 6.0 %collective-permute-done.16 = bf16[512,1024]{1,0:T(8,128)(2,1)S(1)} collective-permute-done((bf16[512,1024]{1,0:T(8,128)(2,1)S(1)}, bf16[512,1024]{1,0:T(8,128)(2,1)S(1)}, u32[]{:S(2)}, u32[]{:S(2)}) %collective-permute-start.16) | collective-permute-done | bytes 1048608 | tf_op jit(solution)/shard_map/ppermute | solution.py:21
  242.2 35.3 %collective-permute-done.24 = bf16[512,1024]{1,0:T(8,128)(2,1)S(1)} collective-permute-done((bf16[512,1024]{1,0:T(8,128)(2,1)S(1)}, bf16[512,1024]{1,0:T(8,128)(2,1)S(1)}, u32[]{:S(2)}, u32[]{:S(2)}) %collective-permute-start.24) | collective-permute-done | bytes 1048608 | tf_op jit(solution)/shard_map/ppermute | solution.py:25
  279.0 6.1 %fusion.7 = f32[1792,1024]{1,0:T(8,128)} fusion(bf16[1024,1792]{1,0:T(8,128)(2,1)S(1)} %pad_maximum_fusion.1, bf16[512,1024]{1,0:T(8,128)(2,1)S(1)} %get-tuple-element.47, bf16[512,1024]{1,0:T(8,128)(2,1)S(1)} %get-tuple-element.46), kind=kOutput, calls=%fused_computation.17 | convolution fusion | flops 3762290688 | bytes 13107200 | tf_op jit(solution)/shard_map/dot_general | solution.py:112
  285.1 3.1 add_convert_fusion.1
  290.8 13.0 %add_add_fusion = f32[1792,1024]{1,0:T(8,128)S(1)} fusion(f32[1792,1024]{1,0:T(8,128)} %fusion.7, f32[1792,1024]{1,0:T(8,128)} %fusion.1, f32[1792,1024]{1,0:T(8,128)} %fusion.3, bf16[1024,1792]{1,0:T(8,128)(2,1)} %copy-done.2, bf16[512,1024]{1,0:T(8,128)(2,1)S(1)} %copy-done.5, bf16[512,1024]{1,0:T(8,128)(2,1)S(1)} %copy-done.4), kind=kOutput, calls=%fused_computation.4 | convolution fusion | flops 3767795712 | bytes 35127296 | tf_op jit(solution)/shard_map/dot_general | solution.py:112
  303.9 6.0 %multiply_reduce_fusion = (f32[1792]{0:T(1024)S(1)}, f32[1,1792,1024]{2,1,0:T(8,128)}) fusion(f32[1792,1024]{1,0:T(8,128)S(1)} %add_add_fusion, f32[1792,1024]{1,0:T(8,128)S(1)} %bitcast.18, f32[1792]{0:T(1024)S(1)} %dynamic-slice_reduce_fusion), kind=kLoop, calls=%fused_computation.3 | loop fusion | flops 25688320 | bytes 22034432 | tf_op jit(solution)/shard_map/reduce_sum | solution.py:121
  309.9 7.1 %psum.7 = f32[1,1792]{1,0:T(1,128)} all-reduce(f32[1,1792]{1,0:T(1,128)S(1)} %broadcast_in_dim.20), channel_id=1, replica_groups=mesh['dp'=4,'row'=2,'col'=4] {'col'}, use_global_device_ids=true, to_apply=%region_1.2 | all-reduce | flops 1792 | bytes 14336 | tf_op jit(solution)/shard_map/psum | solution.py:121
  317.0 3.4 %add_convert_fusion = bf16[512,1024]{1,0:T(8,128)(2,1)} fusion(bf16[512,1024]{1,0:T(8,128)(2,1)} %collective-permute-done.18, f32[512,1024]{1,0:T(8,128)} %fusion.28, bf16[512,1024]{1,0:T(8,128)(2,1)S(1)} %collective-permute-done), kind=kLoop, calls=%fused_computation.24 | loop fusion | flops 2621440 | bytes 5242880 | tf_op jit(solution)/shard_map/convert_element_type | solution.py:120
  (77 shorter events, 44.8 us)
Async XLA Ops:
  5.9 26.7 %collective-permute-start.5 = (bf16[256,1792]{1,0:T(8,128)(2,1)}, bf16[256,1792]{1,0:T(8,128)(2,1)}, u32[]{:S(2)}, u32[]{:S(2)}) collective-permute-start(bf16[256,1792]{1,0:T(8,128)(2,1)} %get-tuple-element.28), channel_id=1, source_target_pairs={{0,8},{8,16},{16,24},{24,0},{1,9},{9,17},{17,25},{25,1},{2,10},{10... | collective-permute-start | bytes 2752520 | tf_op jit(solution)/shard_map/ppermute | solution.py:21
  8.9 84.6 %collective-permute-start.7 = (bf16[256,1792]{1,0:T(8,128)(2,1)}, bf16[256,1792]{1,0:T(8,128)(2,1)}, u32[]{:S(2)}, u32[]{:S(2)}) collective-permute-start(bf16[256,1792]{1,0:T(8,128)(2,1)} %get-tuple-element.29), channel_id=1, source_target_pairs={{0,16},{8,24},{16,0},{24,8},{1,17},{9,25},{17,1},{25,9},{2,18},{10... | collective-permute-start | bytes 2752520 | tf_op jit(solution)/shard_map/ppermute | solution.py:21
  11.6 83.4 %collective-permute-start.19 = (bf16[512,1024]{1,0:T(8,128)(2,1)S(1)}, bf16[512,1024]{1,0:T(8,128)(2,1)}, u32[]{:S(2)}, u32[]{:S(2)}) collective-permute-start(bf16[512,1024]{1,0:T(8,128)(2,1)S(1)} %constant_dynamic-slice_fusion), channel_id=1, source_target_pairs={{0,8},{8,16},{16,24},{24,0},{1,9},{9,17},{17,25},{25,1},{2,10},{10... | collective-permute-start | bytes 3145736 | tf_op jit(solution)/shard_map/ppermute | solution.py:21
  32.6 64.0 %collective-permute-start.12 = (bf16[256,1792]{1,0:T(8,128)(2,1)}, bf16[256,1792]{1,0:T(8,128)(2,1)S(1)}, u32[]{:S(2)}, u32[]{:S(2)}) collective-permute-start(bf16[256,1792]{1,0:T(8,128)(2,1)} %collective-permute-done.5), channel_id=1, source_target_pairs={{0,2},{1,3},{2,0},{3,1},{4,6},{5,7},{6,4},{7,5},{8,10},{9,11},{10,... | collective-permute-start | bytes 2752520 | tf_op jit(solution)/shard_map/ppermute | solution.py:25
  34.3 103.2 %collective-permute-start.1 = (bf16[256,1792]{1,0:T(8,128)(2,1)}, bf16[256,1792]{1,0:T(8,128)(2,1)}, u32[]{:S(2)}, u32[]{:S(2)}) collective-permute-start(bf16[256,1792]{1,0:T(8,128)(2,1)} %get-tuple-element.27), channel_id=1, source_target_pairs={{0,24},{8,0},{16,8},{24,16},{1,25},{9,1},{17,9},{25,17},{2,26},{10... | collective-permute-start | bytes 2752520 | tf_op jit(solution)/shard_map/ppermute | solution.py:21
  36.6 102.5 %collective-permute-start.14 = (bf16[256,1792]{1,0:T(8,128)(2,1)}, bf16[256,1792]{1,0:T(8,128)(2,1)}, u32[]{:S(2)}, u32[]{:S(2)}) collective-permute-start(bf16[256,1792]{1,0:T(8,128)(2,1)} %collective-permute-done.5), channel_id=1, source_target_pairs={{0,1},{1,0},{2,3},{3,2},{4,5},{5,4},{6,7},{7,6},{8,9},{9,8},{10,11... | collective-permute-start | bytes 2752520 | tf_op jit(solution)/shard_map/ppermute | solution.py:25
  93.5 45.5 %collective-permute-start.8 = (bf16[256,1792]{1,0:T(8,128)(2,1)}, bf16[256,1792]{1,0:T(8,128)(2,1)}, u32[]{:S(2)}, u32[]{:S(2)}) collective-permute-start(bf16[256,1792]{1,0:T(8,128)(2,1)} %collective-permute-done.7), channel_id=1, source_target_pairs={{0,2},{1,3},{2,0},{3,1},{4,6},{5,7},{6,4},{7,5},{8,10},{9,11},{10,... | collective-permute-start | bytes 2752520 | tf_op jit(solution)/shard_map/ppermute | solution.py:25
  95.0 24.9 %collective-permute-start.20 = (bf16[512,1024]{1,0:T(8,128)(2,1)}, bf16[512,1024]{1,0:T(8,128)(2,1)S(1)}, u32[]{:S(2)}, u32[]{:S(2)}) collective-permute-start(bf16[512,1024]{1,0:T(8,128)(2,1)} %collective-permute-done.19), channel_id=1, source_target_pairs={{0,4},{4,0},{1,5},{5,1},{2,6},{6,2},{3,7},{7,3},{8,12},{12,8},{9,1... | collective-permute-start | bytes 3145736 | tf_op jit(solution)/shard_map/ppermute | solution.py:25
  96.5 44.0 %collective-permute-start.13 = (bf16[256,1792]{1,0:T(8,128)(2,1)S(1)}, bf16[256,1792]{1,0:T(8,128)(2,1)}, u32[]{:S(2)}, u32[]{:S(2)}) collective-permute-start(bf16[256,1792]{1,0:T(8,128)(2,1)S(1)} %collective-permute-done.12), channel_id=1, source_target_pairs={{0,1},{1,0},{2,3},{3,2},{4,5},{5,4},{6,7},{7,6},{8,9},{9,8},{10,11... | collective-permute-start | bytes 2752520 | tf_op jit(solution)/shard_map/ppermute | solution.py:25
  119.9 42.1 %collective-permute-start.21 = (bf16[512,1024]{1,0:T(8,128)(2,1)}, bf16[512,1024]{1,0:T(8,128)(2,1)S(1)}, u32[]{:S(2)}, u32[]{:S(2)}) collective-permute-start(bf16[512,1024]{1,0:T(8,128)(2,1)} %collective-permute-done.19), channel_id=1, source_target_pairs={{0,8},{8,16},{16,24},{24,0},{1,9},{9,17},{17,25},{25,1},{2,10},{10... | collective-permute-start | bytes 3145736 | tf_op jit(solution)/shard_map/ppermute | solution.py:21
  137.5 179.5 %collective-permute-start = (bf16[512,1024]{1,0:T(8,128)(2,1)}, bf16[512,1024]{1,0:T(8,128)(2,1)S(1)}, u32[]{:S(2)}, u32[]{:S(2)}) collective-permute-start(bf16[512,1024]{1,0:T(8,128)(2,1)} %fusion.30), channel_id=1, source_target_pairs={{0,4},{4,0},{1,5},{5,1},{2,6},{6,2},{3,7},{7,3},{8,12},{12,8},{9,1... | collective-permute-start | bytes 3145736 | tf_op jit(solution)/shard_map/ppermute | solution.py:25
  139.1 23.0 %collective-permute-start.2 = (bf16[256,1792]{1,0:T(8,128)(2,1)}, bf16[256,1792]{1,0:T(8,128)(2,1)S(1)}, u32[]{:S(2)}, u32[]{:S(2)}) collective-permute-start(bf16[256,1792]{1,0:T(8,128)(2,1)} %collective-permute-done.1), channel_id=1, source_target_pairs={{0,2},{1,3},{2,0},{3,1},{4,6},{5,7},{6,4},{7,5},{8,10},{9,11},{10,... | collective-permute-start | bytes 2752520 | tf_op jit(solution)/shard_map/ppermute | solution.py:25
  140.6 22.0 %collective-permute-start.9 = (bf16[256,1792]{1,0:T(8,128)(2,1)}, bf16[256,1792]{1,0:T(8,128)(2,1)S(1)}, u32[]{:S(2)}, u32[]{:S(2)}) collective-permute-start(bf16[256,1792]{1,0:T(8,128)(2,1)} %collective-permute-done.8), channel_id=1, source_target_pairs={{0,1},{1,0},{2,3},{3,2},{4,5},{5,4},{6,7},{7,6},{8,9},{9,8},{10,11... | collective-permute-start | bytes 2752520 | tf_op jit(solution)/shard_map/ppermute | solution.py:25
  143.1 28.3 %collective-permute-start.4 = (bf16[256,1792]{1,0:T(8,128)(2,1)}, bf16[256,1792]{1,0:T(8,128)(2,1)S(1)}, u32[]{:S(2)}, u32[]{:S(2)}) collective-permute-start(bf16[256,1792]{1,0:T(8,128)(2,1)} %collective-permute-done.1), channel_id=1, source_target_pairs={{0,1},{1,0},{2,3},{3,2},{4,5},{5,4},{6,7},{7,6},{8,9},{9,8},{10,11... | collective-permute-start | bytes 2752520 | tf_op jit(solution)/shard_map/ppermute | solution.py:25
  162.0 11.0 %collective-permute-start.3 = (bf16[256,1792]{1,0:T(8,128)(2,1)S(1)}, bf16[256,1792]{1,0:T(8,128)(2,1)S(1)}, u32[]{:S(2)}, u32[]{:S(2)}) collective-permute-start(bf16[256,1792]{1,0:T(8,128)(2,1)S(1)} %collective-permute-done.2), channel_id=1, source_target_pairs={{0,1},{1,0},{2,3},{3,2},{4,5},{5,4},{6,7},{7,6},{8,9},{9,8},{10,11... | collective-permute-start | bytes 2752520 | tf_op jit(solution)/shard_map/ppermute | solution.py:25
  162.0 51.1 %collective-permute-start.22 = (bf16[512,1024]{1,0:T(8,128)(2,1)S(1)}, bf16[512,1024]{1,0:T(8,128)(2,1)S(1)}, u32[]{:S(2)}, u32[]{:S(2)}) collective-permute-start(bf16[512,1024]{1,0:T(8,128)(2,1)S(1)} %collective-permute-done.21), channel_id=1, source_target_pairs={{0,4},{4,0},{1,5},{5,1},{2,6},{6,2},{3,7},{7,3},{8,12},{12,8},{9,1... | collective-permute-start | bytes 3145736 | tf_op jit(solution)/shard_map/ppermute | solution.py:25
  162.6 27.1 %collective-permute-start.23 = (bf16[512,1024]{1,0:T(8,128)(2,1)S(1)}, bf16[512,1024]{1,0:T(8,128)(2,1)S(1)}, u32[]{:S(2)}, u32[]{:S(2)}) collective-permute-start(bf16[512,1024]{1,0:T(8,128)(2,1)S(1)} %collective-permute-done.21), channel_id=1, source_target_pairs={{0,8},{8,16},{16,24},{24,0},{1,9},{9,17},{17,25},{25,1},{2,10},{10... | collective-permute-start | bytes 3145736 | tf_op jit(solution)/shard_map/ppermute | solution.py:21
  171.4 39.1 %collective-permute-start.15 = (bf16[512,1024]{1,0:T(8,128)(2,1)S(1)}, bf16[512,1024]{1,0:T(8,128)(2,1)S(1)}, u32[]{:S(2)}, u32[]{:S(2)}) collective-permute-start(bf16[512,1024]{1,0:T(8,128)(2,1)S(1)} %fusion.39), channel_id=1, source_target_pairs={{0,4},{4,0},{1,5},{5,1},{2,6},{6,2},{3,7},{7,3},{8,12},{12,8},{9,1... | collective-permute-start | bytes 3145736 | tf_op jit(solution)/shard_map/ppermute | solution.py:25
  173.0 60.0 %collective-permute-start.11 = (bf16[512,1024]{1,0:T(8,128)(2,1)S(1)}, bf16[512,1024]{1,0:T(8,128)(2,1)S(1)}, u32[]{:S(2)}, u32[]{:S(2)}) collective-permute-start(bf16[512,1024]{1,0:T(8,128)(2,1)S(1)} %fusion.36), channel_id=1, source_target_pairs={{0,4},{4,0},{1,5},{5,1},{2,6},{6,2},{3,7},{7,3},{8,12},{12,8},{9,1... | collective-permute-start | bytes 3145736 | tf_op jit(solution)/shard_map/ppermute | solution.py:25
  189.7 95.4 %collective-permute-start.6 = (bf16[512,1024]{1,0:T(8,128)(2,1)S(1)}, bf16[512,1024]{1,0:T(8,128)(2,1)S(1)}, u32[]{:S(2)}, u32[]{:S(2)}) collective-permute-start(bf16[512,1024]{1,0:T(8,128)(2,1)S(1)} %fusion.33), channel_id=1, source_target_pairs={{0,4},{4,0},{1,5},{5,1},{2,6},{6,2},{3,7},{7,3},{8,12},{12,8},{9,1... | collective-permute-start | bytes 3145736 | tf_op jit(solution)/shard_map/ppermute | solution.py:25
  210.5 67.0 %collective-permute-start.24 = (bf16[512,1024]{1,0:T(8,128)(2,1)S(1)}, bf16[512,1024]{1,0:T(8,128)(2,1)S(1)}, u32[]{:S(2)}, u32[]{:S(2)}) collective-permute-start(bf16[512,1024]{1,0:T(8,128)(2,1)S(1)} %collective-permute-done.23), channel_id=1, source_target_pairs={{0,4},{4,0},{1,5},{5,1},{2,6},{6,2},{3,7},{7,3},{8,12},{12,8},{9,1... | collective-permute-start | bytes 3145736 | tf_op jit(solution)/shard_map/ppermute | solution.py:25
  213.1 25.8 %collective-permute-start.16 = (bf16[512,1024]{1,0:T(8,128)(2,1)S(1)}, bf16[512,1024]{1,0:T(8,128)(2,1)S(1)}, u32[]{:S(2)}, u32[]{:S(2)}) collective-permute-start(bf16[512,1024]{1,0:T(8,128)(2,1)S(1)} %add_convert_fusion.3), channel_id=1, source_target_pairs={{0,8},{8,16},{16,24},{24,0},{1,9},{9,17},{17,25},{25,1},{2,10},{10... | collective-permute-start | bytes 3145736 | tf_op jit(solution)/shard_map/ppermute | solution.py:21
  241.1 43.9 %collective-permute-start.17 = (bf16[512,1024]{1,0:T(8,128)(2,1)S(1)}, bf16[512,1024]{1,0:T(8,128)(2,1)S(1)}, u32[]{:S(2)}, u32[]{:S(2)}) collective-permute-start(bf16[512,1024]{1,0:T(8,128)(2,1)S(1)} %add_convert_fusion.2), channel_id=1, source_target_pairs={{0,8},{8,16},{16,24},{24,0},{1,9},{9,17},{17,25},{25,1},{2,10},{10... | collective-permute-start | bytes 3145736 | tf_op jit(solution)/shard_map/ppermute | solution.py:21
  288.2 28.8 %collective-permute-start.18 = (bf16[512,1024]{1,0:T(8,128)(2,1)}, bf16[512,1024]{1,0:T(8,128)(2,1)}, u32[]{:S(2)}, u32[]{:S(2)}) collective-permute-start(bf16[512,1024]{1,0:T(8,128)(2,1)} %add_convert_fusion.1), channel_id=1, source_target_pairs={{0,8},{8,16},{16,24},{24,0},{1,9},{9,17},{17,25},{25,1},{2,10},{10... | collective-permute-start | bytes 3145736 | tf_op jit(solution)/shard_map/ppermute | solution.py:21
  (11 other events, 246.8 us)
where the time goes:
time: 321 us; the launch traced here: 320 us
  waiting for transfers between devices  177 us (55%)
  matrix products  59 us (18%)
  starting transfers between devices  46 us (14%)
  other arithmetic  24 us (7%)
  blocking collectives  7.12 us (2%)
  local copies, waits for them, and re-layouts  5.99 us (2%)
    ppermute x16, waiting for transfers between devices, swap(): return lax.ppermute(block, axis, [(i, i ^ bit) for i in range(count)])  95.4 us
    ppermute x9, waiting for transfers between devices, shift(): lax.ppermute(block, axis, [(i, (i + by) % count) for i in range(count)])  82 us
    ppermute x9, starting transfers between devices, shift(): lax.ppermute(block, axis, [(i, (i + by) % count) for i in range(count)])  33 us
    dot_general x3, matrix products, shards(): lax.dot_general(grad, act, (((0,), (0,)), ((), ())), preferred_element_ty...  25.2 us
    dot_general x4, matrix products, reduced(): jnp.dot(kept, quantized, preferred_element_type=jnp.float32)  13.8 us
    ppermute x16, starting transfers between devices, swap(): return lax.ppermute(block, axis, [(i, i ^ bit) for i in range(count)])  13 us
    dot_general x4, matrix products, reduced(): jnp.dot(sent, quantized, preferred_element_type=jnp.float32)  11.9 us
    select_n x6, other arithmetic, gather_rows(): jnp.where(flag, parts[key ^ bit], parts[key])  8.27 us
  transfers between devices with their start and end apart: 25, of which 9 were waited for; matrix products, arithmetic and copies ran while one was open for 25% of the time, Pallas kernels for 0%

commit v1 on v0

--- a/solution.py
+++ b/solution.py
@@ -2,6 +2,8 @@
 import jax.numpy as jnp
 from jax import lax
 from jax.experimental.layout import Layout, with_layout_constraint
+from jax.experimental import pallas as pl
+from jax.experimental.pallas import tpu as pltpu
 from jax.sharding import PartitionSpec as P
 
 D = 4096
@@ -125,8 +127,465 @@
     return shards
 
 
+MESH = pl.DeviceIdType.MESH
+
+
+def flipped(position, bit):
+    return position + bit * (1 - 2 * lax.rem(position // bit, 2))
+
+
+def make_kernel(n_dp, n_row, n_col, tokens, own, width):
+    quarter = tokens // n_col
+    half = tokens // n_row
+    piece = 128
+    pieces = half // piece
+    block = 256
+    factor_scale = 1.0 / (7.0 * width * n_col) ** 0.5
+    bits = []
+    bit = n_col // 2
+    while bit:
+        bits.append(bit)
+        bit //= 2
+
+    def kernel(act, out_grad, weight, steps, input_grad, weight_grad, step_grad,
+               g_buf, a_buf, q_buf, prod, p_send, p_recv, c_send, c_recv, w_buf, s_buf, acc, sg_buf, sg_in,
+               load_sem, w_sem, out_sem, gz_send, g_recv, gx_send, az_send, ay_send, a_recv,
+               p_ssem, p_rsem, c_ssem, c_rsem, sg_ssem, sg_rsem):
+        me = lax.axis_index("dp")
+        row = lax.axis_index("row")
+        col = lax.axis_index("col")
+        partner = 1 - row
+
+        def remote(src, dst, send, recv, where):
+            return pltpu.make_async_remote_copy(
+                src_ref=src, dst_ref=dst, send_sem=send, recv_sem=recv, device_id=where, device_id_type=MESH
+            )
+
+        def rows_of(index, size):
+            return pl.ds(pl.multiple_of(index * size, size), size)
+
+        barrier = pltpu.get_barrier_semaphore()
+        for k in range(1, n_dp):
+            pl.semaphore_signal(barrier, inc=1, device_id={"dp": lax.rem(me + k, n_dp)}, device_id_type=MESH)
+        pl.semaphore_signal(barrier, inc=1, device_id={"row": partner}, device_id_type=MESH)
+        for bit in bits:
+            pl.semaphore_signal(barrier, inc=1, device_id={"col": flipped(col, bit)}, device_id_type=MESH)
+
+        own_columns = pl.ds(pl.multiple_of(me * own, 128), own)
+        load_g = pltpu.make_async_copy(out_grad.at[:, own_columns], g_buf.at[me], load_sem.at[0])
+        load_a = pltpu.make_async_copy(act, a_buf.at[me], load_sem.at[1])
+
+        def load_w(k):
+            return pltpu.make_async_copy(weight.at[0, pl.ds(k * block, block)], w_buf.at[k % 2], w_sem.at[k % 2])
+
+        load_w(0).start()
+        load_w(1).start()
+        load_g.start()
+        load_a.start()
+        pl.semaphore_wait(barrier, n_dp - 1 + 1 + len(bits))
+
+        def send_g(target):
+            columns = pl.ds(pl.multiple_of(target * own, 128), own)
+            return remote(
+                out_grad.at[rows_of(col, quarter), columns], g_buf.at[me, rows_of(col, quarter)],
+                gz_send.at[target], g_recv.at[me, col], {"dp": target},
+            )
+
+        def each_target(fn):
+            for dist in range(1, n_dp):
+                @pl.when(me + dist < n_dp)
+                def _():
+                    fn(me + dist)
+
+                @pl.when(me - dist >= 0)
+                def _():
+                    fn(me - dist)
+
+        each_target(lambda t: send_g(t).start())
+
+        def send_a(source, toward):
+            part = rows_of(row, half)
+            origin = act.at[part] if source is None else a_buf.at[source, part]
+            index = me if source is None else source
+            return remote(
+                origin, a_buf.at[index, part], az_send.at[index, (toward + 1) // 2], a_recv.at[index, row],
+                {"dp": me + toward},
+            )
+
+        def swap_a(source):
+            part = rows_of(row, half)
+            return remote(
+                a_buf.at[source, part], a_buf.at[source, part], ay_send.at[source], a_recv.at[source, row], {"row": partner}
+            )
+
+        def arrived_a(source, which):
+            part = rows_of(which, half)
+            remote(
+                a_buf.at[source, part], a_buf.at[source, part], ay_send.at[source], a_recv.at[source, which], {"row": partner}
+            ).wait_recv()
+
+        @pl.when(me < n_dp - 1)
+        def _():
+            send_a(None, 1).start()
+
+        @pl.when(me > 0)
+        def _():
+            send_a(None, -1).start()
+
+        for k in range(own // 128):
+            values = steps[0:1, pl.ds(pl.multiple_of(me * own + k * 128, 128), 128)]
+            s_buf[pl.ds(k * 128, 128), :] = jnp.transpose(jnp.broadcast_to(values, (128, 128)))
+
+        n_block = own // block
+
+        def ratio_of(k):
+            s = jnp.concatenate([s_buf[pl.ds(k * block, block), :]] * (width // 128), axis=1)
+            return w_buf[k % 2] / s, s
+
+        for k in range(n_block):
+            load_w(k).wait()
+            ratio, s = ratio_of(k)
+            levels = jnp.floor(jnp.clip(ratio, -8.0, 7.0) + 0.5)
+            q_buf[pl.ds(k * block, block), :] = (levels * s).astype(jnp.bfloat16)
+            if k + 2 < n_block:
+                load_w(k + 2).start()
+        load_g.wait()
+
+        def dx_tile(d, start, size):
+            return jnp.dot(
+                g_buf[d, pl.ds(pl.multiple_of(start, size), size), :], q_buf[...], preferred_element_type=jnp.float32
+            )
+
+        def partial(d, i):
+            part = pl.ds(pl.multiple_of(i * piece, piece), piece)
+            return remote(p_send.at[d, part], p_recv.at[d, part], p_ssem.at[d, i], p_rsem.at[d, i], {"row": partner})
+
+        def send_partials(d):
+            def body(i, carry):
+                p_send[d, pl.ds(pl.multiple_of(i * piece, piece), piece), :] = dx_tile(
+                    d, partner * half + i * piece, piece
+                ).astype(jnp.bfloat16)
+                partial(d, i).start()
+                return carry
+
+            lax.fori_loop(0, pieces, body, 0)
+
+        def add_products(d, first=False):
+            def body(k, carry):
+                rows = pl.ds(pl.multiple_of(k * block, block), block)
+                new = lax.dot_general(
+                    g_buf[d, :, rows], a_buf[d], (((0,), (0,)), ((), ())), preferred_element_type=jnp.float32
+                )
+                if first:
+                    prod[rows, :] = new
+                else:
+                    prod[rows, :] = new + prod[rows, :]
+                return carry
+
+            lax.fori_loop(0, n_block, body, 0)
+
+        send_partials(me)
+        load_a.wait()
+
+        upper = me // (n_dp // 2)
+        mirrored = me + upper * (n_dp - 1 - 2 * me)
+
+        def nth(s):
+            d = s + (s - mirrored + n_dp) // n_dp
+            return d + upper * (n_dp - 1 - 2 * d)
+
+        def g_part(d, which):
+            return g_buf.at[d, rows_of(which, quarter)]
+
+        def forward_g(d, which, b, slot):
+            return remote(
+                g_part(d, which), g_part(d, which), gx_send.at[d, slot], g_recv.at[d, which], {"col": flipped(col, bits[b])}
+            )
+
+        def arrived_g(d, which):
+            remote(
+                g_part(d, which), g_part(d, which), gx_send.at[d, 0], g_recv.at[d, which], {"col": flipped(col, bits[0])}
+            ).wait_recv()
+
+        def hypercube(d, on_arrival, on_send):
+            slot = 0
+            held = [col]
+            on_arrival(d, col)
+            for b in range(len(bits)):
+                on_send(d, col, b, slot)
+                slot += 1
+            for b in range(len(bits)):
+                come = [flipped(which, bits[b]) for which in held]
+                for which in come:
+                    on_arrival(d, which)
+                    for later in range(b + 1, len(bits)):
+                        on_send(d, which, later, slot)
+                        slot += 1
+                held += come
+
+        for s in range(n_dp - 1):
+            d = nth(s)
+            hypercube(d, arrived_g, lambda *a: forward_g(*a).start())
+            send_partials(d)
+            if s == 0:
+                add_products(me, first=True)
+
+        def chain(d, slot, i, toward):
+            part = pl.ds(pl.multiple_of(i * piece, piece), piece)
+            return remote(c_send.at[d, part], c_recv.at[slot, part], c_ssem.at[d, i], c_rsem.at[slot, i], {"dp": me + toward})
+
+        def own_sum(d, i):
+            part = pl.ds(pl.multiple_of(i * piece, piece), piece)
+            partial(d, i).wait_recv()
+            acc[...] = dx_tile(d, row * half + i * piece, piece) + p_recv[d, part, :].astype(jnp.float32)
+
+        def add_incoming(slot, i):
+            part = pl.ds(pl.multiple_of(i * piece, piece), piece)
+            remote(
+                c_recv.at[slot, part], c_recv.at[slot, part], c_ssem.at[0, i], c_rsem.at[slot, i], {"row": partner}
+            ).wait_recv()
+            acc[...] = acc[...] + c_recv[slot, part, :].astype(jnp.float32)
+
+        def pass_on(d, toward):
+            def body(i, carry):
+                part = pl.ds(pl.multiple_of(i * piece, piece), piece)
+                own_sum(d, i)
+                has_incoming = me > 0 if toward > 0 else me < n_dp - 1
+
+                @pl.when(has_incoming)
+                def _():
+                    add_incoming(d, i)
+
+                c_send[d, part, :] = acc[...].astype(jnp.bfloat16)
+                if toward > 0:
+                    chain(d, d, i, 1).start()
+                else:
+                    last = (n_dp - 1 - (me - 1 - d)) // (n_dp - 1)
+                    chain(d, d + last * (n_dp - d), i, -1).start()
+                return carry
+
+            lax.fori_loop(0, pieces, body, 0)
+
+        def pass_up(d):
+            @pl.when(me < d)
+            def _():
+                pass_on(d, 1)
+
+        def pass_down(d):
+            @pl.when(me > d)
+            def _():
+                pass_on(d, -1)
+
+        def take_a(k):
+            @pl.when(me - k >= 0)
+            def _():
+                d = me - k
+                arrived_a(d, row)
+
+                @pl.when(me < n_dp - 1)
+                def _():
+                    send_a(d, 1).start()
+
+                swap_a(d).start()
+
+            @pl.when(me + k < n_dp)
+            def _():
+                d = me + k
+                arrived_a(d, row)
+
+                @pl.when(me > 0)
+                def _():
+                    send_a(d, -1).start()
+
+                swap_a(d).start()
+
+        def products_at(k):
+            for sign in (-1, 1):
+                inside = me - k >= 0 if sign < 0 else me + k < n_dp
+
+                @pl.when(inside)
+                def _():
+                    d = me + sign * k
+                    arrived_a(d, partner)
+                    add_products(d)
+
+        mid = n_dp // 2
+        order = [(mid + j, mid - 1 - j) for j in range(n_dp - mid)]
+        order += [(d, n_dp - 1 - d) for d in range(1, mid)]
+        for k in range(1, n_dp):
+            take_a(k)
+            if k > 2:
+                products_at(k - 1)
+            up, down = order[k - 1]
+            pass_up(up)
+            pass_down(down)
+            if k == 2:
+                products_at(1)
+        products_at(n_dp - 1)
+
+        def store(k):
+            return pltpu.make_async_copy(
+                prod.at[pl.ds(k * block, block)], weight_grad.at[0, pl.ds(k * block, block)], out_sem.at[k]
+            )
+
+        load_w(0).start()
+        load_w(1).start()
+        for k in range(n_block):
+            load_w(k).wait()
+            ratio, _ = ratio_of(k)
+            clipped = jnp.clip(ratio, -8.0, 7.0)
+            inside = (ratio >= -8.0) & (ratio <= 7.0)
+            factor = jnp.where(inside, jnp.floor(clipped + 0.5) - ratio, clipped)
+            rows = pl.ds(k * block, block)
+            values = prod[rows, :]
+            share = values * factor
+            lanes = share[:, 0:128]
+            for j in range(1, width // 128):
+                lanes = lanes + share[:, j * 128:(j + 1) * 128]
+            sg_buf[0, :, rows] = jnp.sum(jnp.transpose(lanes), axis=0, keepdims=True) * factor_scale
+            prod[rows, :] = jnp.where(inside, values, 0.0)
+            store(k).start()
+            if k + 2 < n_block:
+                load_w(k + 2).start()
+
+        def swap_steps(b):
+            return remote(sg_buf.at[b], sg_in.at[b], sg_ssem.at[b], sg_rsem.at[b], {"col": flipped(col, bits[b])})
+
+        for b in range(len(bits)):
+            swap_steps(b).start()
+            swap_steps(b).wait_recv()
+            sg_buf[b + 1] = sg_buf[b] + sg_in[b]
+        step_grad[...] = sg_buf[len(bits)]
+
+        def finish(i, carry):
+            part = pl.ds(pl.multiple_of(i * piece, piece), piece)
+            own_sum(me, i)
+
+            @pl.when(me > 0)
+            def _():
+                add_incoming(me, i)
+
+            @pl.when(me < n_dp - 1)
+            def _():
+                add_incoming(n_dp, i)
+
+            input_grad[part, :] = acc[...].astype(jnp.bfloat16)
+            return carry
+
+        lax.fori_loop(0, pieces, finish, 0)
+
+        each_target(lambda t: send_g(t).wait_send())
+        for s in range(n_dp - 1):
+            d = nth(s)
+            hypercube(d, lambda *a: None, lambda *a: forward_g(*a).wait_send())
+            swap_a(d).wait_send()
+
+        @pl.when(me < n_dp - 1)
+        def _():
+            send_a(None, 1).wait_send()
+
+        @pl.when(me > 0)
+        def _():
+            send_a(None, -1).wait_send()
+
+        for k in range(1, n_dp):
+            @pl.when((me - k >= 0) & (me < n_dp - 1))
+            def _():
+                send_a(me - k, 1).wait_send()
+
+            @pl.when((me + k < n_dp) & (me > 0))
+            def _():
+                send_a(me + k, -1).wait_send()
+
+        def drain(d, carry):
+            def each(i, inner):
+                partial(d, i).wait_send()
+
+                @pl.when(me != d)
+                def _():
+                    part = pl.ds(pl.multiple_of(i * piece, piece), piece)
+                    remote(
+                        c_send.at[d, part], c_send.at[d, part], c_ssem.at[d, i], c_rsem.at[d, i], {"row": partner}
+                    ).wait_send()
+
+                return inner
+
+            return lax.fori_loop(0, pieces, each, carry)
+
+        lax.fori_loop(0, n_dp, drain, 0)
+        for b in range(len(bits)):
+            swap_steps(b).wait_send()
+        for k in range(n_block):
+            store(k).wait()
+
+    scratch = [
+        pltpu.VMEM((n_dp, tokens, own), jnp.bfloat16),
+        pltpu.VMEM((n_dp, tokens, width), jnp.bfloat16),
+        pltpu.VMEM((own, width), jnp.bfloat16),
+        pltpu.VMEM((own, width), jnp.float32),
+        pltpu.VMEM((n_dp, half, width), jnp.bfloat16),
+        pltpu.VMEM((n_dp, half, width), jnp.bfloat16),
+        pltpu.VMEM((n_dp, half, width), jnp.bfloat16),
+        pltpu.VMEM((n_dp + 1, half, width), jnp.bfloat16),
+        pltpu.VMEM((2, block, width), jnp.float32),
+        pltpu.VMEM((own, 128), jnp.float32),
+        pltpu.VMEM((piece, width), jnp.float32),
+        pltpu.VMEM((len(bits) + 1, 1, own), jnp.float32),
+        pltpu.VMEM((len(bits), 1, own), jnp.float32),
+        pltpu.SemaphoreType.DMA((2,)),
+        pltpu.SemaphoreType.DMA((2,)),
+        pltpu.SemaphoreType.DMA((own // block,)),
+        pltpu.SemaphoreType.DMA((n_dp,)),
+        pltpu.SemaphoreType.DMA((n_dp, n_col)),
+        pltpu.SemaphoreType.DMA((n_dp, n_col - 1)),
+        pltpu.SemaphoreType.DMA((n_dp, 2)),
+        pltpu.SemaphoreType.DMA((n_dp,)),
+        pltpu.SemaphoreType.DMA((n_dp, n_row)),
+        pltpu.SemaphoreType.DMA((n_dp, pieces)),
+        pltpu.SemaphoreType.DMA((n_dp, pieces)),
+        pltpu.SemaphoreType.DMA((n_dp, pieces)),
+        pltpu.SemaphoreType.DMA((n_dp + 1, pieces)),
+        pltpu.SemaphoreType.DMA((len(bits),)),
+        pltpu.SemaphoreType.DMA((len(bits),)),
+    ]
+    anywhere = pl.BlockSpec(memory_space=pl.ANY)
+    inside = pl.BlockSpec(memory_space=pltpu.VMEM)
+    return pl.pallas_call(
+        kernel,
+        out_shape=(
+            jax.ShapeDtypeStruct((half, width), jnp.bfloat16),
+            jax.ShapeDtypeStruct((1, own, width), jnp.float32),
+            jax.ShapeDtypeStruct((1, own), jnp.float32),
+        ),
+        in_specs=[anywhere, anywhere, anywhere, inside],
+        out_specs=(inside, anywhere, inside),
+        scratch_shapes=scratch,
+        compiler_params=pltpu.CompilerParams(collective_id=0, has_side_effects=True, vmem_limit_bytes=67043328),
+        name="backward",
+    )
+
+
+def fits(n_dp, n_row, n_col, activations, weight):
+    tokens, width = activations.shape
+    own = weight.shape[1]
+    return (
+        n_dp % 2 == 0 and n_row == 2 and n_col > 1 and n_col & (n_col - 1) == 0
+        and own % 256 == 0 and width % 128 == 0 and tokens % (128 * n_row) == 0 and tokens % (16 * n_col) == 0
+        and n_dp * tokens * (own + width) <= 12 * 2**20
+    )
+
+
 def solution(mesh):
+    n_dp, n_row, n_col = mesh.shape["dp"], mesh.shape["row"], mesh.shape["col"]
     in_specs = (P("dp", "col"), P("dp", "row"), P("row", "dp", "col"), P("row", None))
     out_specs = (P(("dp", "row"), "col"), P("row", "dp", "col"), P("row", "dp"))
-    shards = make_shards(mesh.shape["dp"], mesh.shape["row"], mesh.shape["col"])
+    general = make_shards(n_dp, n_row, n_col)
+
+    def shards(activations, out_grad, weight, step_size):
+        if not fits(n_dp, n_row, n_col, activations, weight):
+            return general(activations, out_grad, weight, step_size)
+        tokens, width = activations.shape
+        call = make_kernel(n_dp, n_row, n_col, tokens, weight.shape[1], width)
+        return call(activations, out_grad, weight, step_size)
+
     return jax.shard_map(shards, mesh=mesh, in_specs=in_specs, out_specs=out_specs, check_vma=False)

time: 321 us -> 259 us (0.81)
  Pallas kernels: 0 us -> 247 us
  waiting for transfers between devices: 177 us -> 0 us
  matrix products: 59 us -> 0 us
  starting transfers between devices: 46 us -> 0 us
  other arithmetic: 24 us -> 0 us
  blocking collectives: 7.12 us -> 0 us
  local copies, waits for them, and re-layouts: 5.99 us -> 10.4 us
    pallas_call x0 -> x1, Pallas kernels: none -> 247 us  [shards(): return call(activations, out_grad, weight, step_size)]
    ppermute x25 -> x0, waiting for transfers between devices: 177 us -> none  [the longest x16 95.4 us: swap(): return lax.ppermute(block, axis, [(i, i ^ bit) for i in range(count)])]
    dot_general x12 -> x0, matrix products: 59 us -> none  [the longest x3 25.2 us: shards(): lax.dot_general(grad, act, (((0,), (0,)), ((), ())), preferred_element_ty...]
    ppermute x25 -> x0, starting transfers between devices: 46 us -> none  [the longest x9 33 us: shift(): lax.ppermute(block, axis, [(i, (i + by) % count) for i in range(count)])]
    unnamed x20 -> x5, local copies, waits for them, and re-layouts: 0.05 us -> 10.4 us
    convert_element_type x2 -> x0, other arithmetic: 8.66 us -> none  [the longest x1 5.23 us: quantize(): quantized = (levels * scales[:, None]).astype(jnp.bfloat16)]
    select_n x6 -> x0, other arithmetic: 8.27 us -> none  [gather_rows(): jnp.where(flag, parts[key ^ bit], parts[key])]
    psum x1 -> x0, blocking collectives: 7.12 us -> none  [shards(): lax.psum(jnp.sum(products * factor, axis=1) * grad_factor, 'col')]
  transfers between devices with their start and end apart: 25 -> 0, of which waited for: 9 -> 0; matrix products, arithmetic and copies ran while one was open for 25% -> 0% of each run, Pallas kernels for 0% -> 0%
where the time goes in v1:
time: 259 us; the launch traced here: 258 us
  Pallas kernels  247 us (95%)
  local copies, waits for them, and re-layouts  10.4 us (4%)
    pallas_call x1, Pallas kernels, shards(): return call(activations, out_grad, weight, step_size)  247 us
    unnamed x5, local copies, waits for them, and re-layouts  10.4 us

profile of v1, /device:TPU:0, one launch (start us, length us, event | category | flops | bytes accessed | tf_op | source)
XLA Modules:
  0.0 257.7 jit_solution(7249453465501498634)
XLA Ops:
  0.6 246.6 %backward.1 = (bf16[512,1024]{1,0:T(8,128)(2,1)}, f32[1,1792,1024]{2,1,0:T(8,128)}, f32[1,1792]{1,0:T(1,128)}) custom-call(bf16[1024,1024]{1,0:T(8,128)(2,1)} %act.1, bf16[1024,7168]{1,0:T(8,128)(2,1)} %out_grad.1, f32[1,1792,1024]{2,1,0:T(8,128)} %weight.1, f32[1,7168]{1,0:T(1,128)} %steps.1), custom_call_target="tpu_custom_call" | custom-call | tf_op jit(solution)/shard_map/backward/pallas_call | solution.py:589
  247.3 2.3 copy.10
  249.5 0.0 copy-start
  249.5 7.5 %copy.11 = f32[1,1792,1024]{2,1,0:T(8,128)} copy(f32[1,1792,1024]{2,1,0:T(8,128)} %get-tuple-element.7) | data formatting | bytes 14680064
  257.1 0.0 copy-done
  257.1 0.6 copy.12
Async XLA Ops:
  249.5 7.5 %copy-start = (f32[1,1792]{1,0:T(1,128)S(1)}, f32[1,1792]{1,0:T(1,128)}, u32[]{:S(2)}) copy-start(f32[1,1792]{1,0:T(1,128)} %get-tuple-element.8) | copy-start | bytes 21508

commit v2 on v0

--- a/solution.py
+++ b/solution.py
@@ -2,6 +2,8 @@
 import jax.numpy as jnp
 from jax import lax
 from jax.experimental.layout import Layout, with_layout_constraint
+from jax.experimental import pallas as pl
+from jax.experimental.pallas import tpu as pltpu
 from jax.sharding import PartitionSpec as P
 
 D = 4096
@@ -125,8 +127,444 @@
     return shards
 
 
+MESH = pl.DeviceIdType.MESH
+
+
+def flipped(position, bit):
+    return position + bit * (1 - 2 * lax.rem(position // bit, 2))
+
+
+def make_kernel(n_dp, n_row, n_col, tokens, own, width):
+    quarter = tokens // n_col
+    half = tokens // n_row
+    piece = 128
+    pieces = half // piece
+    block = 256
+    halves = 2
+    g_rows = quarter // halves
+    a_rows = half // halves
+    factor_scale = 1.0 / (7.0 * width * n_col) ** 0.5
+    bits = []
+    bit = n_col // 2
+    while bit:
+        bits.append(bit)
+        bit //= 2
+
+    def kernel(act, out_grad, weight, steps, input_grad, weight_grad, step_grad,
+               g_buf, a_buf, q_buf, f_buf, p_send, p_recv, c_send, c_recv, w_buf, s_buf, acc, sg_buf, sg_in,
+               load_sem, w_sem, gz_send, g_recv, gx_send, az_send, ay_send, a_recv,
+               p_ssem, p_rsem, c_ssem, c_rsem, sg_ssem, sg_rsem):
+        prod = weight_grad.at[0]
+        me = lax.axis_index("dp")
+        row = lax.axis_index("row")
+        col = lax.axis_index("col")
+        partner = 1 - row
+
+        def remote(src, dst, send, recv, where):
+            return pltpu.make_async_remote_copy(
+                src_ref=src, dst_ref=dst, send_sem=send, recv_sem=recv, device_id=where, device_id_type=MESH
+            )
+
+        def rows_of(index, size):
+            return pl.ds(pl.multiple_of(index * size, size), size)
+
+        barrier = pltpu.get_barrier_semaphore()
+        for k in range(1, n_dp):
+            pl.semaphore_signal(barrier, inc=1, device_id={"dp": lax.rem(me + k, n_dp)}, device_id_type=MESH)
+        pl.semaphore_signal(barrier, inc=1, device_id={"row": partner}, device_id_type=MESH)
+        columns_by = [col]
+        for bit in reversed(bits):
+            columns_by += [flipped(which, bit) for which in columns_by]
+        for which in columns_by[1:]:
+            pl.semaphore_signal(barrier, inc=1, device_id={"col": which}, device_id_type=MESH)
+
+        own_columns = pl.ds(pl.multiple_of(me * own, 128), own)
+        load_g = pltpu.make_async_copy(out_grad.at[:, own_columns], g_buf.at[me], load_sem.at[0])
+        load_a = pltpu.make_async_copy(act, a_buf.at[me], load_sem.at[1])
+
+        def load_w(k):
+            return pltpu.make_async_copy(weight.at[0, pl.ds(k * block, block)], w_buf.at[k % 2], w_sem.at[k % 2])
+
+        load_w(0).start()
+        load_w(1).start()
+        load_g.start()
+        load_a.start()
+        pl.semaphore_wait(barrier, n_dp - 1 + 1 + n_col - 1)
+
+        def g_span(which, h):
+            return pl.ds(pl.multiple_of(which * quarter + h * g_rows, g_rows), g_rows)
+
+        def send_g(target, h):
+            columns = pl.ds(pl.multiple_of(target * own, 128), own)
+            return remote(
+                out_grad.at[g_span(col, h), columns], g_buf.at[me, g_span(col, h)],
+                gz_send.at[target, h], g_recv.at[me, col, h], {"dp": target},
+            )
+
+        upper = me // (n_dp // 2)
+
+        def at(position):
+            return position + upper * (n_dp - 1 - 2 * position)
+
+        toward = 1 - 2 * upper
+        place = at(me)
+        spot = [at(position) for position in range(n_dp)]
+        started = ([], [])
+
+        def go(role, make):
+            make().start()
+            started[role].append(make)
+
+        def give_g(role, target):
+            for h in range(halves):
+                go(role, lambda h=h: send_g(target, h))
+
+        @pl.when(place == 0)
+        def _():
+            give_g(0, spot[1])
+
+        @pl.when(place == 1)
+        def _():
+            give_g(1, spot[2])
+            give_g(1, spot[0])
+
+        def a_span(which, h):
+            return pl.ds(pl.multiple_of(which * half + h * a_rows, a_rows), a_rows)
+
+        def send_a(source, inward, h, which, slot, own=False):
+            span = a_span(which, h)
+            return remote(
+                act.at[span] if own else a_buf.at[source, span], a_buf.at[source, span],
+                az_send.at[slot, inward, h], a_recv.at[source, which, h], {"dp": me + (2 * inward - 1) * toward},
+            )
+
+        def swap_a(source, h):
+            span = a_span(row, h)
+            return remote(
+                a_buf.at[source, span], a_buf.at[source, span], ay_send.at[source, h], a_recv.at[source, row, h],
+                {"row": partner},
+            )
+
+        def arrived_a(source, which, h):
+            span = a_span(which, h)
+            remote(
+                a_buf.at[source, span], a_buf.at[source, span], ay_send.at[source, h], a_recv.at[source, which, h],
+                {"row": partner},
+            ).wait_recv()
+
+        def give_a(role, inward, other=False):
+            which, slot = (partner, n_dp) if other else (row, me)
+            for h in range(halves):
+                go(role, lambda h=h: send_a(me, inward, h, which, slot, own=True))
+
+        for k in range(own // 128):
+            values = steps[0:1, pl.ds(pl.multiple_of(me * own + k * 128, 128), 128)]
+            s_buf[pl.ds(k * 128, 128), :] = jnp.transpose(jnp.broadcast_to(values, (128, 128)))
+
+        n_block = own // block
+
+        for k in range(n_block):
+            load_w(k).wait()
+            s = jnp.concatenate([s_buf[pl.ds(k * block, block), :]] * (width // 128), axis=1)
+            ratio = w_buf[k % 2] / s
+            clipped = jnp.clip(ratio, -8.0, 7.0)
+            levels = jnp.floor(clipped + 0.5)
+            q_buf[pl.ds(k * block, block), :] = (levels * s).astype(jnp.bfloat16)
+            f_buf[pl.ds(k * block, block), :] = jnp.where(clipped == ratio, levels - ratio, clipped).astype(jnp.bfloat16)
+            if k + 2 < n_block:
+                load_w(k + 2).start()
+        load_g.wait()
+
+        def dx_tile(d, start, size):
+            return jnp.dot(
+                g_buf[d, pl.ds(pl.multiple_of(start, size), size), :], q_buf[...], preferred_element_type=jnp.float32
+            )
+
+        def partial(d, i):
+            part = pl.ds(pl.multiple_of(i * piece, piece), piece)
+            return remote(p_send.at[d, part], p_recv.at[d, part], p_ssem.at[d, i], p_rsem.at[d, i], {"row": partner})
+
+        def send_partials(d):
+            def body(i, carry):
+                p_send[d, pl.ds(pl.multiple_of(i * piece, piece), piece), :] = dx_tile(
+                    d, partner * half + i * piece, piece
+                ).astype(jnp.bfloat16)
+                partial(d, i).start()
+                return carry
+
+            lax.fori_loop(0, pieces, body, 0)
+
+        def add_products(d, first=False, last=False):
+            def body(k, carry):
+                rows = pl.ds(pl.multiple_of(k * block, block), block)
+                new = lax.dot_general(
+                    g_buf[d, :, rows], a_buf[d], (((0,), (0,)), ((), ())), preferred_element_type=jnp.float32
+                )
+                if not first:
+                    new = new + prod[rows, :]
+                if last:
+                    factor = f_buf[rows, :].astype(jnp.float32)
+                    prod[rows, :] = jnp.where(jnp.abs(factor) < 1.0, new, 0.0)
+                    share = new * factor
+                    lanes = share[:, 0:128]
+                    for j in range(1, width // 128):
+                        lanes = lanes + share[:, j * 128:(j + 1) * 128]
+                    sg_buf[:, rows] = jnp.sum(jnp.transpose(lanes), axis=0, keepdims=True) * factor_scale
+                else:
+                    prod[rows, :] = new
+                return carry
+
+            lax.fori_loop(0, n_block, body, 0)
+
+        send_partials(me)
+        load_a.wait()
+        add_products(me, first=True)
+
+        def forward_g(d, differs, bit, slot, h):
+            span = g_span(columns_by[differs], h)
+            return remote(
+                g_buf.at[d, span], g_buf.at[d, span], gx_send.at[d, slot, h], g_recv.at[d, columns_by[differs], h],
+                {"col": columns_by[bit]},
+            )
+
+        def arrived_g(d, differs, h):
+            forward_g(d, differs, bits[0], 0, h).wait_recv()
+
+        def first_g(role, d, then=None):
+            for h in range(halves):
+                arrived_g(d, 0, h)
+                for slot, bit in enumerate(bits):
+                    go(role, lambda bit=bit, slot=slot, h=h: forward_g(d, 0, bit, slot, h))
+                if h == 0 and then is not None:
+                    then()
+
+        def rest_g(role, d):
+            slot, held = len(bits), [0]
+            for b, bit in enumerate(bits):
+                come = [differs ^ bit for differs in held]
+                for differs in come:
+                    later = bits[b + 1:]
+                    for h in range(halves):
+                        arrived_g(d, differs, h)
+                        for j, over in enumerate(later):
+                            go(role, lambda differs=differs, over=over, slot=slot + j, h=h: forward_g(d, differs, over, slot, h))
+                    slot += len(later)
+                held += come
+            send_partials(d)
+
+        def chain(d, slot, i, step):
+            part = pl.ds(pl.multiple_of(i * piece, piece), piece)
+            return remote(c_send.at[d, part], c_recv.at[slot, part], c_ssem.at[d, i], c_rsem.at[slot, i], {"dp": me + step})
+
+        def own_sum(d, i):
+            part = pl.ds(pl.multiple_of(i * piece, piece), piece)
+            partial(d, i).wait_recv()
+            acc[...] = dx_tile(d, row * half + i * piece, piece) + p_recv[d, part, :].astype(jnp.float32)
+
+        def add_incoming(slot, i):
+            part = pl.ds(pl.multiple_of(i * piece, piece), piece)
+            remote(
+                c_recv.at[slot, part], c_recv.at[slot, part], c_ssem.at[0, i], c_rsem.at[slot, i], {"row": partner}
+            ).wait_recv()
+            acc[...] = acc[...] + c_recv[slot, part, :].astype(jnp.float32)
+
+        def pass_on(d, inward, first=False, last=False):
+            step = toward * (2 * inward - 1)
+            slot = d + (1 - step) // 2 * (n_dp - d) if last else d
+
+            def body(i, carry):
+                part = pl.ds(pl.multiple_of(i * piece, piece), piece)
+                own_sum(d, i)
+                if not first:
+                    add_incoming(d, i)
+                c_send[d, part, :] = acc[...].astype(jnp.bfloat16)
+                chain(d, slot, i, step).start()
+                return carry
+
+            lax.fori_loop(0, pieces, body, 0)
+
+        def take_a(role, d, onward=()):
+            for h in range(halves):
+                arrived_a(d, row, h)
+                for inward in onward:
+                    go(role, lambda inward=inward, h=h: send_a(d, inward, h, row, d))
+                go(role, lambda h=h: swap_a(d, h))
+
+        def products_of(d, both=False, last=False):
+            for which in (row, partner) if both else (partner,):
+                for h in range(halves):
+                    arrived_a(d, which, h)
+            add_products(d, last=last)
+
+        def finish():
+            def body(i, carry):
+                part = pl.ds(pl.multiple_of(i * piece, piece), piece)
+                own_sum(me, i)
+
+                @pl.when(me > 0)
+                def _():
+                    add_incoming(me, i)
+
+                @pl.when(me < n_dp - 1)
+                def _():
+                    add_incoming(n_dp, i)
+
+                input_grad[part, :] = acc[...].astype(jnp.bfloat16)
+                return carry
+
+            lax.fori_loop(0, pieces, body, 0)
+
+        def swap_steps(differs):
+            return remote(
+                sg_buf, sg_in.at[differs - 1], sg_ssem.at[differs - 1], sg_rsem.at[differs - 1],
+                {"col": columns_by[differs]},
+            )
+
+        def give_steps(role):
+            for differs in range(1, n_col):
+                go(role, lambda differs=differs: swap_steps(differs))
+
+        @pl.when(place == 0)
+        def _():
+            r = 0
+            first_g(r, spot[1], lambda: give_g(r, spot[2]))
+            rest_g(r, spot[1])
+            give_a(r, 1)
+            first_g(r, spot[2], lambda: give_g(r, spot[3]))
+            rest_g(r, spot[2])
+            first_g(r, spot[3])
+            pass_on(spot[1], 1, first=True, last=True)
+            rest_g(r, spot[3])
+            pass_on(spot[2], 1, first=True)
+            pass_on(spot[3], 1, first=True)
+            take_a(r, spot[2])
+            products_of(spot[1], both=True)
+            take_a(r, spot[3])
+            products_of(spot[2])
+            products_of(spot[3], last=True)
+            give_steps(r)
+            finish()
+
+        @pl.when(place == 1)
+        def _():
+            r = 1
+            first_g(r, spot[0], lambda: give_a(r, 0))
+            first_g(r, spot[2])
+            give_g(r, spot[3])
+            rest_g(r, spot[0])
+            first_g(r, spot[3])
+            rest_g(r, spot[2])
+            give_a(r, 1)
+            rest_g(r, spot[3])
+            give_a(r, 0, other=True)
+            take_a(r, spot[0], (1,))
+            take_a(r, spot[2], (0,))
+            take_a(r, spot[3], (0,))
+            pass_on(spot[2], 1, last=True)
+            products_of(spot[0])
+            pass_on(spot[3], 1)
+            finish()
+            products_of(spot[2])
+            pass_on(spot[0], 0, last=True)
+            products_of(spot[3], last=True)
+            give_steps(r)
+
+        for differs in range(1, n_col):
+            swap_steps(differs).wait_recv()
+        total = sg_buf[...]
+        for differs in range(1, n_col):
+            total = total + sg_in[differs - 1]
+        step_grad[...] = total
+
+        for role in range(2):
+            @pl.when(place == role)
+            def _():
+                for make in started[role]:
+                    make().wait_send()
+
+        def drain(d, carry):
+            def each(i, inner):
+                partial(d, i).wait_send()
+
+                @pl.when(me != d)
+                def _():
+                    part = pl.ds(pl.multiple_of(i * piece, piece), piece)
+                    remote(
+                        c_send.at[d, part], c_send.at[d, part], c_ssem.at[d, i], c_rsem.at[d, i], {"row": partner}
+                    ).wait_send()
+
+                return inner
+
+            return lax.fori_loop(0, pieces, each, carry)
+
+        lax.fori_loop(0, n_dp, drain, 0)
+    scratch = [
+        pltpu.VMEM((n_dp, tokens, own), jnp.bfloat16),
+        pltpu.VMEM((n_dp, tokens, width), jnp.bfloat16),
+        pltpu.VMEM((own, width), jnp.bfloat16),
+        pltpu.VMEM((own, width), jnp.bfloat16),
+        pltpu.VMEM((n_dp, half, width), jnp.bfloat16),
+        pltpu.VMEM((n_dp, half, width), jnp.bfloat16),
+        pltpu.VMEM((n_dp, half, width), jnp.bfloat16),
+        pltpu.VMEM((n_dp + 1, half, width), jnp.bfloat16),
+        pltpu.VMEM((2, block, width), jnp.float32),
+        pltpu.VMEM((own, 128), jnp.float32),
+        pltpu.VMEM((piece, width), jnp.float32),
+        pltpu.VMEM((1, own), jnp.float32),
+        pltpu.VMEM((n_col - 1, 1, own), jnp.float32),
+        pltpu.SemaphoreType.DMA((2,)),
+        pltpu.SemaphoreType.DMA((2,)),
+        pltpu.SemaphoreType.DMA((n_dp, halves)),
+        pltpu.SemaphoreType.DMA((n_dp, n_col, halves)),
+        pltpu.SemaphoreType.DMA((n_dp, n_col - 1, halves)),
+        pltpu.SemaphoreType.DMA((n_dp + 1, 2, halves)),
+        pltpu.SemaphoreType.DMA((n_dp, halves)),
+        pltpu.SemaphoreType.DMA((n_dp, n_row, halves)),
+        pltpu.SemaphoreType.DMA((n_dp, pieces)),
+        pltpu.SemaphoreType.DMA((n_dp, pieces)),
+        pltpu.SemaphoreType.DMA((n_dp, pieces)),
+        pltpu.SemaphoreType.DMA((n_dp + 1, pieces)),
+        pltpu.SemaphoreType.DMA((n_col - 1,)),
+        pltpu.SemaphoreType.DMA((n_col - 1,)),
+    ]
+    anywhere = pl.BlockSpec(memory_space=pl.ANY)
+    inside = pl.BlockSpec(memory_space=pltpu.VMEM)
+    return pl.pallas_call(
+        kernel,
+        out_shape=(
+            pltpu.VMEM((half, width), jnp.bfloat16),
+            pltpu.VMEM((1, own, width), jnp.float32),
+            pltpu.VMEM((1, own), jnp.float32),
+        ),
+        in_specs=[anywhere, anywhere, anywhere, inside],
+        out_specs=(inside, inside, inside),
+        scratch_shapes=scratch,
+        compiler_params=pltpu.CompilerParams(collective_id=0, has_side_effects=True, vmem_limit_bytes=54 * 2**20),
+        name="backward",
+    )
+
+
+def fits(n_dp, n_row, n_col, activations, weight):
+    tokens, width = activations.shape
+    own = weight.shape[1]
+    return (
+        n_dp == 4 and n_row == 2 and n_col > 1 and n_col & (n_col - 1) == 0
+        and own % 256 == 0 and width % 128 == 0 and tokens % (128 * n_row) == 0 and tokens % (32 * n_col) == 0
+        and n_dp * tokens * (own + width) <= 12 * 2**20
+    )
+
+
 def solution(mesh):
+    n_dp, n_row, n_col = mesh.shape["dp"], mesh.shape["row"], mesh.shape["col"]
     in_specs = (P("dp", "col"), P("dp", "row"), P("row", "dp", "col"), P("row", None))
     out_specs = (P(("dp", "row"), "col"), P("row", "dp", "col"), P("row", "dp"))
-    shards = make_shards(mesh.shape["dp"], mesh.shape["row"], mesh.shape["col"])
+    general = make_shards(n_dp, n_row, n_col)
+
+    def shards(activations, out_grad, weight, step_size):
+        if not fits(n_dp, n_row, n_col, activations, weight):
+            return general(activations, out_grad, weight, step_size)
+        tokens, width = activations.shape
+        call = make_kernel(n_dp, n_row, n_col, tokens, weight.shape[1], width)
+        return call(activations, out_grad, weight, step_size)
+
     return jax.shard_map(shards, mesh=mesh, in_specs=in_specs, out_specs=out_specs, check_vma=False)

time: 321 us -> 201 us (0.63)
  Pallas kernels: 0 us -> 195 us
  waiting for transfers between devices: 177 us -> 0 us
  matrix products: 59 us -> 0 us
  starting transfers between devices: 46 us -> 0 us
  other arithmetic: 24 us -> 0 us
  blocking collectives: 7.12 us -> 0 us
    pallas_call x0 -> x1, Pallas kernels: none -> 195 us  [shards(): return call(activations, out_grad, weight, step_size)]
    ppermute x25 -> x0, waiting for transfers between devices: 177 us -> none  [the longest x16 95.4 us: swap(): return lax.ppermute(block, axis, [(i, i ^ bit) for i in range(count)])]
    dot_general x12 -> x0, matrix products: 59 us -> none  [the longest x3 25.2 us: shards(): lax.dot_general(grad, act, (((0,), (0,)), ((), ())), preferred_element_ty...]
    ppermute x25 -> x0, starting transfers between devices: 46 us -> none  [the longest x9 33 us: shift(): lax.ppermute(block, axis, [(i, (i + by) % count) for i in range(count)])]
    convert_element_type x2 -> x0, other arithmetic: 8.66 us -> none  [the longest x1 5.23 us: quantize(): quantized = (levels * scales[:, None]).astype(jnp.bfloat16)]
    select_n x6 -> x0, other arithmetic: 8.27 us -> none  [gather_rows(): jnp.where(flag, parts[key ^ bit], parts[key])]
    psum x1 -> x0, blocking collectives: 7.12 us -> none  [shards(): lax.psum(jnp.sum(products * factor, axis=1) * grad_factor, 'col')]
    reduce_sum x1 -> x0, other arithmetic: 5.98 us -> none  [shards(): jnp.sum(products * factor, axis=1) * grad_factor]
  transfers between devices with their start and end apart: 25 -> 0, of which waited for: 9 -> 0; matrix products, arithmetic and copies ran while one was open for 25% -> 0% of each run, Pallas kernels for 0% -> 0%
where the time goes in v2:
time: 201 us
  Pallas kernels  195 us (97%)
  local copies, waits for them, and re-layouts  4.61 us (2%)
    pallas_call x1, Pallas kernels, shards(): return call(activations, out_grad, weight, step_size)  195 us
    unnamed x3, local copies, waits for them, and re-layouts  4.61 us

profile of v2, /device:TPU:0, one launch (start us, length us, event | category | flops | bytes accessed | tf_op | source)
XLA Modules:
  0.0 200.6 jit_solution(8952317274089667791)
XLA Ops:
  0.6 195.3 %backward.1 = (bf16[512,1024]{1,0:T(8,128)(2,1)S(1)}, f32[1,1792,1024]{2,1,0:T(8,128)S(1)}, f32[1,1792]{1,0:T(1,128)S(1)}) custom-call(bf16[1024,1024]{1,0:T(8,128)(2,1)} %act.1, bf16[1024,7168]{1,0:T(8,128)(2,1)} %out_grad.1, f32[1,1792,1024]{2,1,0:T(8,128)} %weight.1, f32[1,7168]{1,0:T(1,128)} %steps.1), custom_call_target="tpu_custom_call" | custom-call | tf_op jit(solution)/shard_map/backward/pallas_call | solution.py:568
  196.0 1.0 copy.10
  196.9 0.6 copy.12
  197.5 3.0 %copy.11 = f32[1,1792,1024]{2,1,0:T(8,128)} copy(f32[1,1792,1024]{2,1,0:T(8,128)S(1)} %get-tuple-element.4) | data formatting | bytes 14680064

commit v3 on v2

--- a/solution.py
+++ b/solution.py
@@ -252,10 +252,9 @@
                 {"row": partner},
             ).wait_recv()
 
-        def give_a(role, inward, other=False):
-            which, slot = (partner, n_dp) if other else (row, me)
+        def give_a(role, inward):
             for h in range(halves):
-                go(role, lambda h=h: send_a(me, inward, h, which, slot, own=True))
+                go(role, lambda h=h: send_a(me, inward, h, row, me, own=True))
 
         for k in range(own // 128):
             values = steps[0:1, pl.ds(pl.multiple_of(me * own + k * 128, 128), 128)]
@@ -368,32 +367,36 @@
             ).wait_recv()
             acc[...] = acc[...] + c_recv[slot, part, :].astype(jnp.float32)
 
-        def pass_on(d, inward, first=False, last=False):
+        def pass_step(i, d, inward, first=False, last=False):
             step = toward * (2 * inward - 1)
             slot = d + (1 - step) // 2 * (n_dp - d) if last else d
-
+            part = pl.ds(pl.multiple_of(i * piece, piece), piece)
+            own_sum(d, i)
+            if not first:
+                add_incoming(d, i)
+            c_send[d, part, :] = acc[...].astype(jnp.bfloat16)
+            chain(d, slot, i, step).start()
+
+        def pass_on(low, high, *jobs):
             def body(i, carry):
-                part = pl.ds(pl.multiple_of(i * piece, piece), piece)
-                own_sum(d, i)
-                if not first:
-                    add_incoming(d, i)
-                c_send[d, part, :] = acc[...].astype(jnp.bfloat16)
-                chain(d, slot, i, step).start()
+                for d, inward, lag, kind in jobs:
+                    pass_step(i - lag, d, inward, **kind)
                 return carry
 
-            lax.fori_loop(0, pieces, body, 0)
-
-        def take_a(role, d, onward=()):
-            for h in range(halves):
+            lax.fori_loop(low, high, body, 0)
+
+        def take_a(role, d, onward=(), swaps=tuple(range(halves)), parts=tuple(range(halves))):
+            for h in parts:
                 arrived_a(d, row, h)
                 for inward in onward:
                     go(role, lambda inward=inward, h=h: send_a(d, inward, h, row, d))
-                go(role, lambda h=h: swap_a(d, h))
-
-        def products_of(d, both=False, last=False):
-            for which in (row, partner) if both else (partner,):
-                for h in range(halves):
-                    arrived_a(d, which, h)
+                if h in swaps:
+                    go(role, lambda h=h: swap_a(d, h))
+
+        def products_of(d, last=False, skip=()):
+            for h in range(halves):
+                if h not in skip:
+                    arrived_a(d, partner, h)
             add_products(d, last=last)
 
         def finish():
@@ -423,6 +426,8 @@
         def give_steps(role):
             for differs in range(1, n_col):
                 go(role, lambda differs=differs: swap_steps(differs))
+
+        start, end, split = dict(first=True), dict(last=True), pieces // 2
 
         @pl.when(place == 0)
         def _():
@@ -431,14 +436,18 @@
             rest_g(r, spot[1])
             give_a(r, 1)
             first_g(r, spot[2], lambda: give_g(r, spot[3]))
+            take_a(r, spot[1], swaps=(0,))
+            go(r, lambda: send_a(me, 1, 0, partner, n_dp, own=True))
             rest_g(r, spot[2])
             first_g(r, spot[3])
-            pass_on(spot[1], 1, first=True, last=True)
             rest_g(r, spot[3])
-            pass_on(spot[2], 1, first=True)
-            pass_on(spot[3], 1, first=True)
-            take_a(r, spot[2])
-            products_of(spot[1], both=True)
+            pass_on(0, split, (spot[2], 1, 0, start))
+            pass_on(0, pieces - 1, (spot[3], 1, 0, start))
+            take_a(r, spot[2], swaps=(1,))
+            pass_on(pieces - 1, pieces, (spot[3], 1, 0, start))
+            pass_on(split, pieces, (spot[2], 1, 0, start))
+            pass_on(0, pieces, (spot[1], 1, 0, dict(first=True, last=True)))
+            products_of(spot[1])
             take_a(r, spot[3])
             products_of(spot[2])
             products_of(spot[3], last=True)
@@ -456,18 +465,25 @@
             rest_g(r, spot[2])
             give_a(r, 1)
             rest_g(r, spot[3])
-            give_a(r, 0, other=True)
-            take_a(r, spot[0], (1,))
+            go(r, lambda: send_a(me, 0, 1, partner, n_dp, own=True))
+            take_a(r, spot[0], (1,), swaps=(1,))
             take_a(r, spot[2], (0,))
-            take_a(r, spot[3], (0,))
-            pass_on(spot[2], 1, last=True)
+            take_a(r, spot[3], (0,), parts=(0,))
+            pass_on(0, split, (spot[2], 1, 0, end))
             products_of(spot[0])
-            pass_on(spot[3], 1)
-            finish()
-            products_of(spot[2])
-            pass_on(spot[0], 0, last=True)
+            take_a(r, spot[3], (0,), parts=(1,))
+            pass_on(0, 1, (spot[3], 1, 0, {}))
+            arrived_a(spot[2], partner, 0)
+            go(r, lambda: send_a(spot[2], 0, 0, partner, n_dp))
+            pass_on(1, split, (spot[3], 1, 0, {}))
+            products_of(spot[2], skip=(0,))
+            pass_on(split, pieces, (spot[3], 1, 0, {}), (spot[0], 0, split, end))
+            pass_on(split, pieces - 1, (spot[0], 0, 0, end))
+            pass_on(split, pieces, (spot[2], 1, 0, end))
+            pass_on(pieces - 1, pieces, (spot[0], 0, 0, end))
             products_of(spot[3], last=True)
             give_steps(r)
+            finish()
 
         for differs in range(1, n_col):
             swap_steps(differs).wait_recv()
@@ -539,7 +555,7 @@
         in_specs=[anywhere, anywhere, anywhere, inside],
         out_specs=(inside, inside, inside),
         scratch_shapes=scratch,
-        compiler_params=pltpu.CompilerParams(collective_id=0, has_side_effects=True, vmem_limit_bytes=54 * 2**20),
+        compiler_params=pltpu.CompilerParams(collective_id=0, has_side_effects=True, vmem_limit_bytes=55 * 2**20),
         name="backward",
     )
 

time: 201 us -> 188 us (0.935)
  Pallas kernels: 195 us -> 182 us
    pallas_call x1, Pallas kernels: 195 us -> 182 us  [shards(): return call(activations, out_grad, weight, step_size)]
where the time goes in v3:
time: 188 us; the launch traced here: 187 us
  Pallas kernels  182 us (97%)
  local copies, waits for them, and re-layouts  4.61 us (2%)
    pallas_call x1, Pallas kernels, shards(): return call(activations, out_grad, weight, step_size)  182 us
    unnamed x3, local copies, waits for them, and re-layouts  4.61 us

profile of v3, /device:TPU:0, one launch (start us, length us, event | category | flops | bytes accessed | tf_op | source)
XLA Modules:
  0.0 187.4 jit_solution(7030389672616150258)
XLA Ops:
  0.6 182.1 %backward.1 = (bf16[512,1024]{1,0:T(8,128)(2,1)S(1)}, f32[1,1792,1024]{2,1,0:T(8,128)S(1)}, f32[1,1792]{1,0:T(1,128)S(1)}) custom-call(bf16[1024,1024]{1,0:T(8,128)(2,1)} %act.1, bf16[1024,7168]{1,0:T(8,128)(2,1)} %out_grad.1, f32[1,1792,1024]{2,1,0:T(8,128)} %weight.1, f32[1,7168]{1,0:T(1,128)} %steps.1), custom_call_target="tpu_custom_call" | custom-call | tf_op jit(solution)/shard_map/backward/pallas_call | solution.py:584
  182.8 1.0 copy.10
  183.7 0.6 copy.12
  184.3 3.0 %copy.11 = f32[1,1792,1024]{2,1,0:T(8,128)} copy(f32[1,1792,1024]{2,1,0:T(8,128)S(1)} %get-tuple-element.4) | data formatting | bytes 14680064

commit v4 on v3

--- a/solution.py
+++ b/solution.py
@@ -142,7 +142,9 @@
     block = 256
     halves = 2
     g_rows = quarter // halves
-    a_rows = half // halves
+    parts = 4
+    a_rows = half // parts
+    block_pieces = quarter // piece
     factor_scale = 1.0 / (7.0 * width * n_col) ** 0.5
     bits = []
     bit = n_col // 2
@@ -192,7 +194,11 @@
         pl.semaphore_wait(barrier, n_dp - 1 + 1 + n_col - 1)
 
         def g_span(which, h):
-            return pl.ds(pl.multiple_of(which * quarter + h * g_rows, g_rows), g_rows)
+            dealt = lax.rem(which, 2) * (n_col // 2) + which // 2
+            return pl.ds(pl.multiple_of(dealt * quarter + h * g_rows, g_rows), g_rows)
+
+        def nth(i):
+            return lax.rem(i + col // 2 * block_pieces, pieces)
 
         def send_g(target, h):
             columns = pl.ds(pl.multiple_of(target * own, 128), own)
@@ -253,7 +259,7 @@
             ).wait_recv()
 
         def give_a(role, inward):
-            for h in range(halves):
+            for h in range(parts):
                 go(role, lambda h=h: send_a(me, inward, h, row, me, own=True))
 
         for k in range(own // 128):
@@ -283,15 +289,16 @@
             part = pl.ds(pl.multiple_of(i * piece, piece), piece)
             return remote(p_send.at[d, part], p_recv.at[d, part], p_ssem.at[d, i], p_rsem.at[d, i], {"row": partner})
 
-        def send_partials(d):
-            def body(i, carry):
+        def send_partials(d, low=0, high=pieces):
+            def body(k, carry):
+                i = nth(k)
                 p_send[d, pl.ds(pl.multiple_of(i * piece, piece), piece), :] = dx_tile(
                     d, partner * half + i * piece, piece
                 ).astype(jnp.bfloat16)
                 partial(d, i).start()
                 return carry
 
-            lax.fori_loop(0, pieces, body, 0)
+            lax.fori_loop(low, high, body, 0)
 
         def add_products(d, first=False, last=False):
             def body(k, carry):
@@ -337,6 +344,11 @@
                 if h == 0 and then is not None:
                     then()
 
+        def early_g(d):
+            for h in range(halves):
+                arrived_g(d, 1, h)
+            send_partials(d, 0, block_pieces)
+
         def rest_g(role, d):
             slot, held = len(bits), [0]
             for b, bit in enumerate(bits):
@@ -344,12 +356,13 @@
                 for differs in come:
                     later = bits[b + 1:]
                     for h in range(halves):
-                        arrived_g(d, differs, h)
+                        if differs != 1:
+                            arrived_g(d, differs, h)
                         for j, over in enumerate(later):
                             go(role, lambda differs=differs, over=over, slot=slot + j, h=h: forward_g(d, differs, over, slot, h))
                     slot += len(later)
                 held += come
-            send_partials(d)
+            send_partials(d, block_pieces)
 
         def chain(d, slot, i, step):
             part = pl.ds(pl.multiple_of(i * piece, piece), piece)
@@ -380,13 +393,13 @@
         def pass_on(low, high, *jobs):
             def body(i, carry):
                 for d, inward, lag, kind in jobs:
-                    pass_step(i - lag, d, inward, **kind)
+                    pass_step(nth(i - lag), d, inward, **kind)
                 return carry
 
             lax.fori_loop(low, high, body, 0)
 
-        def take_a(role, d, onward=(), swaps=tuple(range(halves)), parts=tuple(range(halves))):
-            for h in parts:
+        def take_a(role, d, onward=(), swaps=tuple(range(parts)), which=tuple(range(parts))):
+            for h in which:
                 arrived_a(d, row, h)
                 for inward in onward:
                     go(role, lambda inward=inward, h=h: send_a(d, inward, h, row, d))
@@ -394,13 +407,14 @@
                     go(role, lambda h=h: swap_a(d, h))
 
         def products_of(d, last=False, skip=()):
-            for h in range(halves):
+            for h in range(parts):
                 if h not in skip:
                     arrived_a(d, partner, h)
             add_products(d, last=last)
 
         def finish():
-            def body(i, carry):
+            def body(k, carry):
+                i = nth(k)
                 part = pl.ds(pl.multiple_of(i * piece, piece), piece)
                 own_sum(me, i)
 
@@ -428,27 +442,38 @@
                 go(role, lambda differs=differs: swap_steps(differs))
 
         start, end, split = dict(first=True), dict(last=True), pieces // 2
+        low, high = tuple(range(parts // 2)), tuple(range(parts // 2, parts))
 
         @pl.when(place == 0)
         def _():
             r = 0
             first_g(r, spot[1], lambda: give_g(r, spot[2]))
+            early_g(spot[1])
             rest_g(r, spot[1])
             give_a(r, 1)
-            first_g(r, spot[2], lambda: give_g(r, spot[3]))
-            take_a(r, spot[1], swaps=(0,))
-            go(r, lambda: send_a(me, 1, 0, partner, n_dp, own=True))
+
+            def meanwhile():
+                give_g(r, spot[3])
+                take_a(r, spot[1], which=low)
+
+            first_g(r, spot[2], meanwhile)
+            early_g(spot[2])
+            for h in low:
+                go(r, lambda h=h: send_a(me, 1, h, partner, n_dp, own=True))
             rest_g(r, spot[2])
             first_g(r, spot[3])
+            early_g(spot[3])
             rest_g(r, spot[3])
             pass_on(0, split, (spot[2], 1, 0, start))
             pass_on(0, pieces - 1, (spot[3], 1, 0, start))
-            take_a(r, spot[2], swaps=(1,))
+            take_a(r, spot[2], swaps=tuple(range(1, parts)))
             pass_on(pieces - 1, pieces, (spot[3], 1, 0, start))
             pass_on(split, pieces, (spot[2], 1, 0, start))
             pass_on(0, pieces, (spot[1], 1, 0, dict(first=True, last=True)))
+            take_a(r, spot[3], which=low)
+            take_a(r, spot[1], swaps=(), which=high)
             products_of(spot[1])
-            take_a(r, spot[3])
+            take_a(r, spot[3], which=high)
             products_of(spot[2])
             products_of(spot[3], last=True)
             give_steps(r)
@@ -460,18 +485,22 @@
             first_g(r, spot[0], lambda: give_a(r, 0))
             first_g(r, spot[2])
             give_g(r, spot[3])
+            early_g(spot[0])
+            early_g(spot[2])
             rest_g(r, spot[0])
             first_g(r, spot[3])
+            early_g(spot[3])
             rest_g(r, spot[2])
             give_a(r, 1)
             rest_g(r, spot[3])
-            go(r, lambda: send_a(me, 0, 1, partner, n_dp, own=True))
-            take_a(r, spot[0], (1,), swaps=(1,))
+            for h in high:
+                go(r, lambda h=h: send_a(me, 0, h, partner, n_dp, own=True))
+            take_a(r, spot[0], (1,), swaps=high)
             take_a(r, spot[2], (0,))
-            take_a(r, spot[3], (0,), parts=(0,))
+            take_a(r, spot[3], (0,), which=low)
             pass_on(0, split, (spot[2], 1, 0, end))
             products_of(spot[0])
-            take_a(r, spot[3], (0,), parts=(1,))
+            take_a(r, spot[3], (0,), which=high)
             pass_on(0, 1, (spot[3], 1, 0, {}))
             arrived_a(spot[2], partner, 0)
             go(r, lambda: send_a(spot[2], 0, 0, partner, n_dp))
@@ -533,9 +562,9 @@
         pltpu.SemaphoreType.DMA((n_dp, halves)),
         pltpu.SemaphoreType.DMA((n_dp, n_col, halves)),
         pltpu.SemaphoreType.DMA((n_dp, n_col - 1, halves)),
-        pltpu.SemaphoreType.DMA((n_dp + 1, 2, halves)),
-        pltpu.SemaphoreType.DMA((n_dp, halves)),
-        pltpu.SemaphoreType.DMA((n_dp, n_row, halves)),
+        pltpu.SemaphoreType.DMA((n_dp + 1, 2, parts)),
+        pltpu.SemaphoreType.DMA((n_dp, parts)),
+        pltpu.SemaphoreType.DMA((n_dp, n_row, parts)),
         pltpu.SemaphoreType.DMA((n_dp, pieces)),
         pltpu.SemaphoreType.DMA((n_dp, pieces)),
         pltpu.SemaphoreType.DMA((n_dp, pieces)),
@@ -560,12 +589,38 @@
     )
 
 
+def leave(input_grad, weight_grad, step_grad):
+    held = (input_grad, weight_grad, step_grad)
+    cuts = 8
+    rows = weight_grad.shape[1] // cuts
+
+    def kernel(a, b, c, a_out, b_out, c_out, sems):
+        copies = [pltpu.make_async_copy(a, a_out, sems.at[cuts]), pltpu.make_async_copy(c, c_out, sems.at[cuts + 1])]
+        for k in range(cuts):
+            span = pl.ds(k * rows, rows)
+            copies.append(pltpu.make_async_copy(b.at[:, span], b_out.at[:, span], sems.at[k]))
+        for copy in copies:
+            copy.start()
+        for copy in copies:
+            copy.wait()
+
+    return pl.pallas_call(
+        kernel,
+        out_shape=tuple(jax.ShapeDtypeStruct(x.shape, x.dtype) for x in held),
+        in_specs=[pl.BlockSpec(memory_space=pltpu.VMEM)] * len(held),
+        out_specs=tuple(pl.BlockSpec(memory_space=pl.ANY) for _ in held),
+        scratch_shapes=[pltpu.SemaphoreType.DMA((cuts + 2,))],
+        compiler_params=pltpu.CompilerParams(vmem_limit_bytes=2**20),
+        name="leave",
+    )(*(pltpu.with_memory_space_constraint(x, pltpu.VMEM) for x in held))
+
+
 def fits(n_dp, n_row, n_col, activations, weight):
     tokens, width = activations.shape
     own = weight.shape[1]
     return (
         n_dp == 4 and n_row == 2 and n_col > 1 and n_col & (n_col - 1) == 0
-        and own % 256 == 0 and width % 128 == 0 and tokens % (128 * n_row) == 0 and tokens % (32 * n_col) == 0
+        and own % 256 == 0 and width % 128 == 0 and tokens % (256 * n_row) == 0 and tokens % (128 * n_col) == 0
         and n_dp * tokens * (own + width) <= 12 * 2**20
     )
 
@@ -581,6 +636,6 @@
             return general(activations, out_grad, weight, step_size)
         tokens, width = activations.shape
         call = make_kernel(n_dp, n_row, n_col, tokens, weight.shape[1], width)
-        return call(activations, out_grad, weight, step_size)
+        return leave(*call(activations, out_grad, weight, step_size))
 
     return jax.shard_map(shards, mesh=mesh, in_specs=in_specs, out_specs=out_specs, check_vma=False)

time: 188 us -> 182 us (0.968)
  local copies, waits for them, and re-layouts: 4.61 us -> 0 us
    unnamed x3 -> x0, local copies, waits for them, and re-layouts: 4.61 us -> none
    pallas_call x1 -> x2, Pallas kernels: 182 us -> 181 us  [the longest x1 177 us: shards(): return leave(*call(activations, out_grad, weight, step_size))]
where the time goes in v4:
time: 182 us; the launch traced here: 181 us
  Pallas kernels  181 us (99%)
    pallas_call x1, Pallas kernels, shards(): return leave(*call(activations, out_grad, weight, step_size))  177 us

profile of v4, /device:TPU:0, one launch (start us, length us, event | category | flops | bytes accessed | tf_op | source)
XLA Modules:
  0.0 181.5 jit_solution(11462389728162057348)
XLA Ops:
  0.6 177.3 %backward.1 = (bf16[512,1024]{1,0:T(8,128)(2,1)S(1)}, f32[1,1792,1024]{2,1,0:T(8,128)S(1)}, f32[1,1792]{1,0:T(1,128)S(1)}) custom-call(bf16[1024,1024]{1,0:T(8,128)(2,1)} %act.1, bf16[1024,7168]{1,0:T(8,128)(2,1)} %out_grad.1, f32[1,1792,1024]{2,1,0:T(8,128)} %weight.1, f32[1,7168]{1,0:T(1,128)} %steps.1), custom_call_target="tpu_custom_call" | custom-call | tf_op jit(solution)/shard_map/backward/pallas_call | solution.py:639
  177.9 3.4 %leave.1 = (bf16[512,1024]{1,0:T(8,128)(2,1)}, f32[1,1792,1024]{2,1,0:T(8,128)}, f32[1,1792]{1,0:T(1,128)}) custom-call(bf16[512,1024]{1,0:T(8,128)(2,1)S(1)} %get-tuple-element.6.a, f32[1,1792,1024]{2,1,0:T(8,128)S(1)} %get-tuple-element.7.b, f32[1,1792]{1,0:T(1,128)S(1)} %get-tuple-element.8.c), custom_call_target="tpu_custom_call" | custom-call | tf_op jit(solution)/shard_map/leave/pallas_call | solution.py:607

commit v5 on v4

--- a/solution.py
+++ b/solution.py
@@ -287,7 +287,7 @@
 
         def partial(d, i):
             part = pl.ds(pl.multiple_of(i * piece, piece), piece)
-            return remote(p_send.at[d, part], p_recv.at[d, part], p_ssem.at[d, i], p_rsem.at[d, i], {"row": partner})
+            return remote(p_send.at[d, part], p_recv.at[d, part], p_ssem.at[d], p_rsem.at[d, i], {"row": partner})
 
         def send_partials(d, low=0, high=pieces):
             def body(k, carry):
@@ -366,7 +366,7 @@
 
         def chain(d, slot, i, step):
             part = pl.ds(pl.multiple_of(i * piece, piece), piece)
-            return remote(c_send.at[d, part], c_recv.at[slot, part], c_ssem.at[d, i], c_rsem.at[slot, i], {"dp": me + step})
+            return remote(c_send.at[d, part], c_recv.at[slot, part], c_ssem.at[d], c_rsem.at[slot, i], {"dp": me + step})
 
         def own_sum(d, i):
             part = pl.ds(pl.multiple_of(i * piece, piece), piece)
@@ -376,7 +376,7 @@
         def add_incoming(slot, i):
             part = pl.ds(pl.multiple_of(i * piece, piece), piece)
             remote(
-                c_recv.at[slot, part], c_recv.at[slot, part], c_ssem.at[0, i], c_rsem.at[slot, i], {"row": partner}
+                c_recv.at[slot, part], c_recv.at[slot, part], c_ssem.at[0], c_rsem.at[slot, i], {"row": partner}
             ).wait_recv()
             acc[...] = acc[...] + c_recv[slot, part, :].astype(jnp.float32)
 
@@ -466,7 +466,7 @@
             rest_g(r, spot[3])
             pass_on(0, split, (spot[2], 1, 0, start))
             pass_on(0, pieces - 1, (spot[3], 1, 0, start))
-            take_a(r, spot[2], swaps=tuple(range(1, parts)))
+            take_a(r, spot[2])
             pass_on(pieces - 1, pieces, (spot[3], 1, 0, start))
             pass_on(split, pieces, (spot[2], 1, 0, start))
             pass_on(0, pieces, (spot[1], 1, 0, dict(first=True, last=True)))
@@ -502,10 +502,8 @@
             products_of(spot[0])
             take_a(r, spot[3], (0,), which=high)
             pass_on(0, 1, (spot[3], 1, 0, {}))
-            arrived_a(spot[2], partner, 0)
-            go(r, lambda: send_a(spot[2], 0, 0, partner, n_dp))
             pass_on(1, split, (spot[3], 1, 0, {}))
-            products_of(spot[2], skip=(0,))
+            products_of(spot[2])
             pass_on(split, pieces, (spot[3], 1, 0, {}), (spot[0], 0, split, end))
             pass_on(split, pieces - 1, (spot[0], 0, 0, end))
             pass_on(split, pieces, (spot[2], 1, 0, end))
@@ -528,19 +526,13 @@
                     make().wait_send()
 
         def drain(d, carry):
-            def each(i, inner):
-                partial(d, i).wait_send()
-
-                @pl.when(me != d)
-                def _():
-                    part = pl.ds(pl.multiple_of(i * piece, piece), piece)
-                    remote(
-                        c_send.at[d, part], c_send.at[d, part], c_ssem.at[d, i], c_rsem.at[d, i], {"row": partner}
-                    ).wait_send()
-
-                return inner
-
-            return lax.fori_loop(0, pieces, each, carry)
+            remote(p_send.at[d], p_send.at[d], p_ssem.at[d], p_rsem.at[d, 0], {"row": partner}).wait_send()
+
+            @pl.when(me != d)
+            def _():
+                remote(c_send.at[d], c_send.at[d], c_ssem.at[d], c_rsem.at[d, 0], {"row": partner}).wait_send()
+
+            return carry
 
         lax.fori_loop(0, n_dp, drain, 0)
     scratch = [
@@ -565,9 +557,9 @@
         pltpu.SemaphoreType.DMA((n_dp + 1, 2, parts)),
         pltpu.SemaphoreType.DMA((n_dp, parts)),
         pltpu.SemaphoreType.DMA((n_dp, n_row, parts)),
+        pltpu.SemaphoreType.DMA((n_dp,)),
         pltpu.SemaphoreType.DMA((n_dp, pieces)),
-        pltpu.SemaphoreType.DMA((n_dp, pieces)),
-        pltpu.SemaphoreType.DMA((n_dp, pieces)),
+        pltpu.SemaphoreType.DMA((n_dp,)),
         pltpu.SemaphoreType.DMA((n_dp + 1, pieces)),
         pltpu.SemaphoreType.DMA((n_col - 1,)),
         pltpu.SemaphoreType.DMA((n_col - 1,)),

time: 182 us -> 181 us (level)
  no operation moved by 1% of the time
where the time goes in v5:
time: 181 us
  Pallas kernels  180 us (99%)
    pallas_call x1, Pallas kernels, shards(): return leave(*call(activations, out_grad, weight, step_size))  177 us

profile of v5, /device:TPU:0, one launch (start us, length us, event | category | flops | bytes accessed | tf_op | source)
XLA Modules:
  0.0 181.2 jit_solution(13976259047955526013)
XLA Ops:
  0.6 177.0 %backward.1 = (bf16[512,1024]{1,0:T(8,128)(2,1)S(1)}, f32[1,1792,1024]{2,1,0:T(8,128)S(1)}, f32[1,1792]{1,0:T(1,128)S(1)}) custom-call(bf16[1024,1024]{1,0:T(8,128)(2,1)} %act.1, bf16[1024,7168]{1,0:T(8,128)(2,1)} %out_grad.1, f32[1,1792,1024]{2,1,0:T(8,128)} %weight.1, f32[1,7168]{1,0:T(1,128)} %steps.1), custom_call_target="tpu_custom_call" | custom-call | tf_op jit(solution)/shard_map/backward/pallas_call | solution.py:631
  177.6 3.4 %leave.1 = (bf16[512,1024]{1,0:T(8,128)(2,1)}, f32[1,1792,1024]{2,1,0:T(8,128)}, f32[1,1792]{1,0:T(1,128)}) custom-call(bf16[512,1024]{1,0:T(8,128)(2,1)S(1)} %get-tuple-element.6.a, f32[1,1792,1024]{2,1,0:T(8,128)S(1)} %get-tuple-element.7.b, f32[1,1792]{1,0:T(1,128)S(1)} %get-tuple-element.8.c), custom_call_target="tpu_custom_call" | custom-call | tf_op jit(solution)/shard_map/leave/pallas_call | solution.py:599
